TPU v7x, 32 devices: a whole 2x2x4 slice. The times are simulated.
32 devices in a mesh: dp: 32 (over z, y, x, core).
Axes of the slice: x: 2, y: 2, z: 4, core: 2. Of those that a mesh axis runs over, the one named last changes fastest.
Arguments:
- grad_rows: bfloat16 [32, 7520256], P('dp')
- master: float32 [7520256], P('dp')
- mom_first: float32 [7520256], P('dp')
- mom_second: float32 [7520256], P('dp')
- decay_mask: int32 [7520256], P('dp')
- learn_rate: float32 [1], replicated
Outputs:
- output 1: bfloat16 [7520256], replicated
- output 2: float32 [7520256], P('dp')
- output 3: float32 [7520256], P('dp')
- output 4: float32 [7520256], P('dp')
- output 5: float32 [1], replicated
All inputs are finite; a program needn't handle non-finite values.
Results may differ from a plain program's by a relative error of at most 0.001.
Values are sent between devices in bfloat16 or wider.
A program may use at most 1 GiB of HBM per device.

v0:
```python
import jax
import jax.numpy as jnp
from jax import lax
from jax.sharding import PartitionSpec as P, NamedSharding

BETA_FIRST = 0.9
BETA_SECOND = 0.95
ADAM_EPS = 1e-8
CLIP_EPS = 1e-6
WEIGHT_DECAY = 0.1
ADAM_STEP = 10


def adamw_block(grad_mean, grad_norm, master, mom_first, mom_second, decay_mask, learn_rate):
    clip_coef = jnp.minimum(1.0, 1.0 / (grad_norm + CLIP_EPS))
    clipped = grad_mean * clip_coef
    new_first = BETA_FIRST * mom_first + (1.0 - BETA_FIRST) * clipped
    new_second = BETA_SECOND * mom_second + (1.0 - BETA_SECOND) * clipped * clipped
    step_dir = (new_first / (1.0 - BETA_FIRST ** ADAM_STEP)) / (jnp.sqrt(new_second / (1.0 - BETA_SECOND ** ADAM_STEP)) + ADAM_EPS)
    decay_flag = decay_mask.astype(jnp.float32)
    new_master = master - learn_rate[0] * (step_dir + WEIGHT_DECAY * decay_flag * master)
    return new_master, new_first, new_second


def solution(mesh):
    num_dev = mesh.shape['dp']

    def local_step(grad_row, master, mom_first, mom_second, decay_mask, learn_rate):
        shard_len = master.shape[0]
        grad_parts = grad_row.reshape(num_dev, shard_len)
        received = lax.all_to_all(grad_parts, 'dp', 0, 0, tiled=True)
        grad_mean = jnp.sum(received, axis=0, dtype=jnp.float32) / num_dev
        sq_total = lax.psum(jnp.sum(grad_mean * grad_mean), 'dp')
        grad_norm = jnp.sqrt(sq_total)
        new_master, new_first, new_second = adamw_block(grad_mean, grad_norm, master, mom_first, mom_second, decay_mask, learn_rate)
        params = lax.all_gather(new_master.astype(jnp.bfloat16), 'dp', tiled=True)
        return params, new_master, new_first, new_second, grad_norm.reshape(1)

    return jax.shard_map(local_step, mesh=mesh, in_specs=(P('dp', None), P('dp'), P('dp'), P('dp'), P('dp'), P()), out_specs=(P(), P('dp'), P('dp'), P('dp'), P()), check_vma=False)
```

profile of v0, /device:TPU:0, one launch (start us, length us, event | category | flops | bytes accessed | tf_op | source)
XLA Modules:
  0.0 1292.3 jit_solution(12729299353028457676)
XLA Ops:
  7.2 0.0 all-gather.3.cloned.1.call-start
  7.2 0.5 broadcast.13
  7.7 299.3 %reduce.2 = bf16[32,235008]{1,0:T(8,128)(2,1)} reduce(bf16[32,1,235008]{2,1,0:T(2,128)(2,1)} %bitcast.4, bf16[]{:T(256)} %broadcast.13), dimensions={1}, to_apply=%bitcast.1.reduce_sub_computation | reduce | bytes 30081026 | tf_op jit(solution)/shard_map/all_to_all | solution.py:31
  307.0 11.7 reshape.22
  318.8 341.1 %all_to_all.9 = bf16[32,2,117504]{2,1,0:T(2,128)(2,1)} all-to-all(bf16[32,2,117504]{2,1,0:T(2,128)(2,1)} %reshape.22), channel_id=1, replica_groups=mesh['dp'=32] {'dp'}, dimensions={0} | all-to-all | bytes 30081024 | tf_op jit(solution)/shard_map/all_to_all | solution.py:31
  659.8 0.0 copy-start
  659.9 0.0 copy-start.1
  659.9 37.4 %reshape.23 = bf16[32,1,235008]{2,1,0:T(2,128)(2,1)} reshape(bf16[32,2,117504]{2,1,0:T(2,128)(2,1)} %all_to_all.9) | data formatting | bytes 30081024
  697.2 33.4 %convert_reduce_fusion = f32[235008]{0:T(1024)S(1)} fusion(bf16[32,1,235008]{2,1,0:T(2,128)(2,1)} %reshape.23), kind=kLoop, calls=%fused_computation | loop fusion | flops 14805504 | bytes 15980544 | tf_op jit(solution)/shard_map/reduce_sum | solution.py:32
  730.7 0.8 multiply_reduce_fusion
  732.1 39.5 %psum.7 = f32[]{:T(128)} all-reduce(f32[]{:T(128)} %multiply_reduce_fusion), channel_id=1, replica_groups=mesh['dp'=32] {'dp'}, use_global_device_ids=true, to_apply=%region_2.0 | all-reduce | flops 1 | bytes 8 | tf_op jit(solution)/shard_map/psum | solution.py:33
  772.4 0.0 copy-done
  772.4 0.0 copy-done.1
  772.4 3.6 fusion.1
  776.0 6.1 reshape.19
  782.1 0.0 all-gather.3.cloned.1.call-update
  782.1 177.4 %all-gather.3.cloned.1.call-done = bf16[32,1,235008]{2,1,0:T(2,128)(2,1)} async-done(((bf16[1,1,235008]{2,1,0:T(2,128)(2,1)}), bf16[32,1,235008]{2,1,0:T(2,128)(2,1)}) %all-gather.3.cloned.1.call-update) | async-done | bytes 15040528 | tf_op jit(solution)/shard_map/all_gather | solution.py:36
  959.5 298.5 %reduce.1 = bf16[32,235008]{1,0:T(8,128)(2,1)} reduce(bf16[32,1,235008]{2,1,0:T(2,128)(2,1)} %all-gather.3.cloned.1.call-done, bf16[]{:T(256)} %constant.26), dimensions={1}, to_apply=%all-gather.reduce_sub_computation | reduce | bytes 30081026 | tf_op jit(solution)/shard_map/all_gather | solution.py:36
  1258.0 26.3 %reshape.20 = bf16[7520256]{0:T(1024)(128)(2,1)} reshape(bf16[32,235008]{1,0:T(8,128)(2,1)} %reduce.1) | data formatting | bytes 30081024
Async XLA Ops:
  7.2 952.3 %all-gather.3.cloned.1.call-start = ((), (), s32[]{:S(2)}) async-start(), calls=%async_computation.1 | async-start | bytes 31021056 | tf_op jit(solution)/shard_map/all_gather | solution.py:36
  659.8 112.5 %copy-start = (f32[235008]{0:T(1024)S(1)}, f32[235008]{0:T(1024)}, u32[]{:S(2)}) copy-start(f32[235008]{0:T(1024)} %param.7) | copy-start | bytes 2820100
  659.9 112.5 %copy-start.1 = (s32[235008]{0:T(1024)S(1)}, s32[235008]{0:T(1024)}, u32[]{:S(2)}) copy-start(s32[235008]{0:T(1024)} %param.10) | copy-start | bytes 2820100
Sparse Core Ops, SparseCore 0:
  782.2 177.2 all-gather.2
where the time goes:
time: 1290 us
  other arithmetic  636 us (49%)
  blocking collectives  381 us (30%)
  waiting for transfers between devices  177 us (14%)
  local copies, waits for them, and re-layouts  82.1 us (6%)
  between operations  16.6 us (1%)
    all_to_all x1, blocking collectives, local_step(): received = lax.all_to_all(grad_parts, 'dp', 0, 0, tiled=True)  341 us
    all_to_all x1, other arithmetic, local_step(): received = lax.all_to_all(grad_parts, 'dp', 0, 0, tiled=True)  299 us
    all_gather x1, other arithmetic, local_step(): params = lax.all_gather(new_master.astype(jnp.bfloat16), 'dp', tiled=True)  299 us
    all_gather x1, waiting for transfers between devices, local_step(): params = lax.all_gather(new_master.astype(jnp.bfloat16), 'dp', tiled=True)  177 us
    unnamed x8, local copies, waits for them, and re-layouts  81.5 us
    psum x1, blocking collectives, local_step(): sq_total = lax.psum(jnp.sum(grad_mean * grad_mean), 'dp')  39.5 us
    reduce_sum x1, other arithmetic, local_step(): grad_mean = jnp.sum(received, axis=0, dtype=jnp.float32) / num_dev  33.4 us
  transfers between devices with their start and end apart: 1, of which 1 were waited for; matrix products, arithmetic and copies ran while one was open for 0% of the time, Pallas kernels for 0%

commit v1 on v0

v1 whole, which is shorter than its diff:
```python
import functools

import jax
import jax.numpy as jnp
from jax import lax
from jax.experimental import pallas as pl
from jax.experimental.pallas import tpu as pltpu
from jax.sharding import PartitionSpec as P

BETA_FIRST = 0.9
BETA_SECOND = 0.95
ADAM_EPS = 1e-8
CLIP_EPS = 1e-6
WEIGHT_DECAY = 0.1
ADAM_STEP = 10
LANES = 128
TILE = 16
STAGES = 3
MESH = pl.DeviceIdType.MESH
F32 = jnp.float32
BF16 = jnp.bfloat16


def over_tiles(count, group, body):
    whole = count // group
    size = group * TILE

    def step(i, carry):
        body(pl.multiple_of(i * size, size), size)
        return carry

    if whole:
        lax.fori_loop(0, whole, step, 0)
    if count % group:
        body(whole * size, (count % group) * TILE)


def kernel(rows, grad_hbm, w_hbm, m_hbm, v_hbm, d_hbm, lr_ref,
           out_hbm, nw_hbm, nm_hbm, nv_hbm, norm_ref,
           stage0, stage1, stage2, row, got1, kept, sent2, got2, got3, w, m, v, d, own, part1, part2,
           stage_sem, state_sem, s1, r1, s2, r2, s3, r3, ns1, nr1, ns2, nr2, gs1, gr1, gs2, gr2, gs3, gr3, gs4, gr4):
    stages = (stage0, stage1, stage2)
    tiles = -(-rows // TILE)
    tiles_c = (tiles - tiles // 2, tiles // 2)
    rows_c = (tiles_c[0] * TILE, tiles_c[1] * TILE)
    first_c = (0, rows_c[0])
    block = rows * LANES
    units = rows // 2
    unit_first = (0, rows_c[0] // 2)
    unit_len = (rows_c[0] // 2, units - rows_c[0] // 2)
    full = rows // TILE
    rest = rows - full * TILE

    me = lax.axis_index('dp')
    z = lax.div(me, 8)
    me8 = lax.rem(me, 8)
    y = lax.div(me8, 4)
    x = lax.rem(lax.div(me8, 2), 2)
    c = lax.rem(me8, 2)

    def flip(a, by):
        return 1 - a if by else a

    def in_plane(jy, jx, jc):
        return flip(y, jy) * 4 + flip(x, jx) * 2 + flip(c, jc)

    def peer(jy, jx, jc):
        return z * 8 + in_plane(jy, jx, jc)

    def z_ahead(g):
        return lax.rem(z + 1 + g, 4)

    def z_behind(g):
        return lax.rem(z + 3 - g, 4)

    plane = [(jy, jx, jc) for jy in (0, 1) for jx in (0, 1) for jc in (0, 1) if jy + jx + jc]

    def state_copy(i):
        return pltpu.make_async_copy((w_hbm, m_hbm, v_hbm, d_hbm)[i], (w, m, v, d)[i], state_sem.at[i])

    order = [(1, 1, 1), (1, 1, 0), (1, 0, 1), (1, 0, 0), (0, 1, 1), (0, 1, 0), (0, 0, 1), (0, 0, 0)]
    work = [(g, j) for g in range(4) for j in order]

    def block_of(g, j):
        return z_ahead(g) * 8 + in_plane(*j)

    def stage_copy(i):
        g, j = work[i]
        at = pl.multiple_of(block_of(g, j) * block, LANES)
        return pltpu.make_async_copy(grad_hbm.at[:, pl.ds(at, block)], stages[i % STAGES], stage_sem.at[i % STAGES])

    for i in range(STAGES):
        stage_copy(i).start()

    barrier = pltpu.get_barrier_semaphore()
    for j in plane:
        pl.semaphore_signal(barrier, inc=1, device_id=(peer(*j),), device_id_type=MESH)
    for g in range(3):
        pl.semaphore_signal(barrier, inc=1, device_id=(z_ahead(g) * 8 + me8,), device_id_type=MESH)

    def pack(i):
        g, j = work[i]
        k = block_of(g, j)
        source = stages[i % STAGES]
        stage_copy(i).wait()

        def body(at, size):
            lane = at * LANES
            if not isinstance(at, int):
                lane = pl.multiple_of(lane, TILE * LANES)
            val = source[:, pl.ds(lane, size * LANES)].astype(F32).reshape(size, LANES)
            row[k, pl.ds(at, size), :] = val.astype(BF16)

        over_tiles(full, 4, body)
        if rest:
            row[k, pl.ds(full * TILE, TILE), :] = jnp.zeros((TILE, LANES), BF16)
            body(full * TILE, rest)
        if i + STAGES < len(work):
            stage_copy(i + STAGES).start()

    def first_copy(col, g, j2, slot):
        near = 1 if slot else 0
        jc = 1 if slot != 1 else 0
        j = (j2, near, jc) if col == 0 else (near, j2, jc)
        to = peer(0, near, jc) if col == 0 else peer(near, 0, jc)
        return pltpu.make_async_remote_copy(
            src_ref=row.at[block_of(g, j), pl.ds(first_c[col], rows_c[col])],
            dst_ref=got1.at[col, g, j2, slot, pl.ds(0, rows_c[col])],
            send_sem=s1.at[col, g, j2, slot], recv_sem=r1.at[col, g, j2, slot],
            device_id=(to,), device_id_type=MESH)

    def second_copy(col, g):
        to = peer(1, 0, 0) if col == 0 else peer(0, 1, 0)
        return pltpu.make_async_remote_copy(
            src_ref=sent2.at[col, g, pl.ds(0, rows_c[col])], dst_ref=got2.at[col, g, pl.ds(0, rows_c[col])],
            send_sem=s2.at[col, g], recv_sem=r2.at[col, g], device_id=(to,), device_id_type=MESH)

    def third_copy(col, g):
        return pltpu.make_async_remote_copy(
            src_ref=kept.at[col, g, pl.ds(0, rows_c[col])], dst_ref=got3.at[col, g, pl.ds(0, rows_c[col])],
            send_sem=s3.at[col, g], recv_sem=r3.at[col, g],
            device_id=(z_ahead(g) * 8 + me8,), device_id_type=MESH)

    def send_first(g, j2):
        for slot in (1, 2, 0):
            for col in (0, 1):
                first_copy(col, g, j2, slot).start()

    def four_sum(col, g, j2, target):
        for slot in (0, 1, 2):
            first_copy(col, g, j2, slot).wait_recv()
        k = block_of(g, (j2, 0, 0) if col == 0 else (0, j2, 0))

        def body(at, size):
            near = pl.ds(at, size)
            mine = row[k, pl.ds(first_c[col] + at, size), :].astype(F32) + got1[col, g, j2, 0, near, :].astype(F32)
            other = got1[col, g, j2, 1, near, :].astype(F32) + got1[col, g, j2, 2, near, :].astype(F32)
            target[col, g, near, :] = mine + other

        over_tiles(tiles_c[col], 4, body)

    for i in range(8):
        pack(i)
        if i == 0:
            pl.semaphore_wait(barrier, 10)
        if i == 5:
            send_first(0, 1)
    send_first(0, 0)
    for i in range(4):
        state_copy(i).start()
    for i in range(8, 16):
        pack(i)

    for g in range(4):
        for col in (0, 1):
            four_sum(col, g, 1, sent2)
        for col in (0, 1):
            second_copy(col, g).start()
        if g < 3:
            send_first(g + 1, 1)
        for col in (0, 1):
            four_sum(col, g, 0, kept)
        if g < 3:
            send_first(g + 1, 0)
        if g < 2:
            for i in range(8 * (g + 2), 8 * (g + 3)):
                pack(i)
        for col in (0, 1):
            second_copy(col, g).wait_recv()

            if g < 3:
                def body(at, size):
                    kept[col, g, pl.ds(at, size), :] = kept[col, g, pl.ds(at, size), :] + got2[col, g, pl.ds(at, size), :]

                over_tiles(tiles_c[col], 4, body)
        if g < 3:
            for col in (0, 1):
                third_copy(col, g).start()

    for i in range(4):
        state_copy(i).wait()
    acc = jnp.zeros((8, LANES), F32)
    for col in (0, 1):
        for g in range(3):
            third_copy(col, g).wait_recv()

        def mean_of(at, size):
            near = pl.ds(at, size)
            total = (kept[col, 3, near, :] + got2[col, 3, near, :]) + (got3[col, 0, near, :] + got3[col, 1, near, :])
            total = (total + got3[col, 2, near, :]) * (1.0 / 32.0)
            kept[col, 3, near, :] = total
            return jnp.sum((total * total).reshape(size // 8, 8, LANES), axis=0)

        whole = tiles_c[col] // 4
        if whole:
            acc = lax.fori_loop(0, whole, lambda i, a: a + mean_of(pl.multiple_of(i * 64, 64), 64), acc)
        if tiles_c[col] % 4:
            acc = acc + mean_of(whole * 64, (tiles_c[col] % 4) * TILE)

    def norm_copy1(j):
        return pltpu.make_async_remote_copy(
            src_ref=part1.at[me8], dst_ref=part1.at[me8],
            send_sem=ns1.at[j], recv_sem=nr1.at[j], device_id=(peer(*plane[j]),), device_id_type=MESH)

    def norm_copy2(g):
        return pltpu.make_async_remote_copy(
            src_ref=part2.at[z], dst_ref=part2.at[z],
            send_sem=ns2.at[g], recv_sem=nr2.at[g], device_id=(z_ahead(g) * 8 + me8,), device_id_type=MESH)

    def landed(ref, at, send_sem, recv_sem):
        return pltpu.make_async_remote_copy(
            src_ref=ref.at[at], dst_ref=ref.at[at], send_sem=send_sem, recv_sem=recv_sem,
            device_id=(me,), device_id_type=MESH)

    part1[me8] = acc
    for j in range(7):
        norm_copy1(j).start()
    for j in range(7):
        landed(part1, in_plane(*plane[j]), ns1.at[j], nr1.at[j]).wait_recv()
    acc = part1[0]
    for j in range(1, 8):
        acc = acc + part1[j]
    part2[z] = acc
    for g in range(3):
        norm_copy2(g).start()
    for g in range(3):
        landed(part2, z_behind(g), ns2.at[g], nr2.at[g]).wait_recv()
    acc = (part2[0] + part2[1]) + (part2[2] + part2[3])
    norm = jnp.sqrt(jnp.full((1, LANES), jnp.sum(acc), F32))
    norm_ref[...] = norm
    coef = jnp.minimum(1.0, 1.0 / (norm + CLIP_EPS))
    lr = lr_ref[0]

    def update(col):
        def body(at, size):
            near = pl.ds(first_c[col] + at, size)
            h = kept[col, 3, pl.ds(at, size), :] * coef
            nm = BETA_FIRST * m[near, :] + (1.0 - BETA_FIRST) * h
            nv = BETA_SECOND * v[near, :] + (1.0 - BETA_SECOND) * h * h
            step = (nm * (1.0 / (1.0 - BETA_FIRST ** ADAM_STEP))) / (jnp.sqrt(nv * (1.0 / (1.0 - BETA_SECOND ** ADAM_STEP))) + ADAM_EPS)
            old = w[near, :]
            nw = old - lr * (step + WEIGHT_DECAY * d[near, :].astype(F32) * old)
            m[near, :] = nm
            v[near, :] = nv
            w[near, :] = nw
            unit = first_c[col] // 2 + (at // 2 if isinstance(at, int) else lax.div(at, 2))
            own[pl.ds(unit, size // 2)] = nw.astype(BF16).reshape(size // 2, 2, LANES)

        count = tiles_c[col] if col == 0 else tiles_c[col] - (1 if rest else 0)
        over_tiles(count, 2, body)
        if col == 1 and rest:
            body(count * TILE, rest)

    def place(zz, jy, jx, jc, col):
        k = zz * 8 + in_plane(jy, jx, jc)
        return out_hbm.at[pl.ds(k * units + unit_first[col], unit_len[col])]

    def zed(zi):
        return z if zi == 3 else z_behind(zi)

    def mine_or(zi, spot, col, first):
        return own.at[pl.ds(unit_first[col], unit_len[col])] if first else spot

    def gather1(col, g):
        spot = place(z, 0, 0, 0, col)
        return pltpu.make_async_remote_copy(
            src_ref=mine_or(3, spot, col, True), dst_ref=spot, send_sem=gs1.at[col, g], recv_sem=gr1.at[col, g],
            device_id=(z_ahead(g) * 8 + me8,), device_id_type=MESH)

    def gather2(col, zi):
        spot = place(zed(zi), 0, 0, 0, col)
        to = peer(1, 0, 0) if col == 0 else peer(0, 1, 0)
        return pltpu.make_async_remote_copy(
            src_ref=mine_or(zi, spot, col, zi == 3), dst_ref=spot, send_sem=gs2.at[col, zi], recv_sem=gr2.at[col, zi],
            device_id=(to,), device_id_type=MESH)

    def gather3(col, zi, j2):
        spot = place(zed(zi), j2, 0, 0, col) if col == 0 else place(zed(zi), 0, j2, 0, col)
        to = peer(0, 1, 0) if col == 0 else peer(1, 0, 0)
        return pltpu.make_async_remote_copy(
            src_ref=mine_or(zi, spot, col, zi == 3 and j2 == 0), dst_ref=spot,
            send_sem=gs3.at[col, zi, j2], recv_sem=gr3.at[col, zi, j2], device_id=(to,), device_id_type=MESH)

    def gather4(col, zi, j2, j3):
        spot = place(zed(zi), j2, j3, 0, col) if col == 0 else place(zed(zi), j3, j2, 0, col)
        return pltpu.make_async_remote_copy(
            src_ref=mine_or(zi, spot, col, zi == 3 and j2 == 0 and j3 == 0), dst_ref=spot,
            send_sem=gs4.at[col, zi, j2, j3], recv_sem=gr4.at[col, zi, j2, j3],
            device_id=(peer(0, 0, 1),), device_id_type=MESH)

    for col in (0, 1):
        update(col)
        gather1(col, 0).start()
        gather2(col, 3).start()
        gather3(col, 3, 0).start()
    for g in (1, 2):
        for col in (0, 1):
            gather1(col, g).start()
    results = [pltpu.make_async_copy((w, m, v)[i], (nw_hbm, nm_hbm, nv_hbm)[i], state_sem.at[i]) for i in range(3)]
    results.append(pltpu.make_async_copy(own, out_hbm.at[pl.ds(me * units, units)], state_sem.at[3]))
    for copy in results:
        copy.start()
    for col in (0, 1):
        gather4(col, 3, 0, 0).start()

    def landed1(col, g):
        return pltpu.make_async_remote_copy(
            src_ref=own.at[pl.ds(unit_first[col], unit_len[col])], dst_ref=place(z_behind(g), 0, 0, 0, col),
            send_sem=gs1.at[col, g], recv_sem=gr1.at[col, g], device_id=(me,), device_id_type=MESH)

    for zi in (3, 0, 1, 2):
        if zi < 3:
            for col in (0, 1):
                landed1(col, zi).wait_recv()
                gather2(col, zi).start()
                gather3(col, zi, 0).start()
                gather4(col, zi, 0, 0).start()
        for col in (0, 1):
            gather2(col, zi).wait_recv()
            gather3(col, zi, 1).start()
            gather4(col, zi, 1, 0).start()
    for zi in (3, 0, 1, 2):
        for j2 in (0, 1):
            for col in (0, 1):
                gather3(col, zi, j2).wait_recv()
                gather4(col, zi, j2, 1).start()

    for copy in results:
        copy.wait()
    for col in (0, 1):
        for zi in (3, 0, 1, 2):
            for j2 in (0, 1):
                for j3 in (0, 1):
                    gather4(col, zi, j2, j3).wait()
                gather3(col, zi, j2).wait_send()
            gather2(col, zi).wait_send()
        for g in range(3):
            gather1(col, g).wait_send()
            third_copy(col, g).wait_send()
        for g in range(4):
            second_copy(col, g).wait_send()
            for j2 in (0, 1):
                for slot in range(3):
                    first_copy(col, g, j2, slot).wait_send()
    for j in range(7):
        norm_copy1(j).wait_send()
    for g in range(3):
        norm_copy2(g).wait_send()


def solution(mesh):
    num_dev = mesh.shape['dp']

    def local_step(grad_row, master, mom_first, mom_second, decay_mask, learn_rate):
        shard_len = master.shape[0]
        rows = shard_len // LANES
        tiles = -(-rows // TILE)
        half = (tiles - tiles // 2) * TILE
        dma = pltpu.SemaphoreType.DMA
        any_spec = pl.BlockSpec(memory_space=pl.ANY)
        flat = (rows, LANES)
        state = jax.ShapeDtypeStruct(flat, F32)
        outs = pl.pallas_call(
            functools.partial(kernel, rows),
            out_shape=(jax.ShapeDtypeStruct((num_dev * rows // 2, 2, LANES), BF16), state, state, state,
                       jax.ShapeDtypeStruct((1, LANES), F32)),
            in_specs=[any_spec] * 5 + [pl.BlockSpec(memory_space=pltpu.SMEM)],
            out_specs=(any_spec, any_spec, any_spec, any_spec, pl.BlockSpec(memory_space=pltpu.VMEM)),
            scratch_shapes=[pltpu.VMEM((1, shard_len), BF16)] * STAGES + [
                pltpu.VMEM((num_dev, tiles * TILE, LANES), BF16),
                pltpu.VMEM((2, 4, 2, 3, half, LANES), BF16),
                pltpu.VMEM((2, 4, half, LANES), F32),
                pltpu.VMEM((2, 4, half, LANES), F32),
                pltpu.VMEM((2, 4, half, LANES), F32),
                pltpu.VMEM((2, 3, half, LANES), F32),
                pltpu.VMEM(flat, F32), pltpu.VMEM(flat, F32), pltpu.VMEM(flat, F32), pltpu.VMEM(flat, jnp.int32),
                pltpu.VMEM((rows // 2, 2, LANES), BF16),
                pltpu.VMEM((8, 8, LANES), F32), pltpu.VMEM((4, 8, LANES), F32),
                dma((STAGES,)), dma((4,)),
                dma((2, 4, 2, 3)), dma((2, 4, 2, 3)), dma((2, 4)), dma((2, 4)), dma((2, 3)), dma((2, 3)),
                dma((7,)), dma((7,)), dma((3,)), dma((3,)),
                dma((2, 3)), dma((2, 3)), dma((2, 4)), dma((2, 4)), dma((2, 4, 2)), dma((2, 4, 2)),
                dma((2, 4, 2, 2)), dma((2, 4, 2, 2)),
            ],
            compiler_params=pltpu.CompilerParams(
                collective_id=0, has_side_effects=True, vmem_limit_bytes=60 * 1024 * 1024),
        )(grad_row, master.reshape(flat), mom_first.reshape(flat), mom_second.reshape(flat), decay_mask.reshape(flat), learn_rate)
        params, new_master, new_first, new_second, norm = outs
        return (params.reshape(num_dev * shard_len), new_master.reshape(shard_len), new_first.reshape(shard_len),
                new_second.reshape(shard_len), norm[0, :1])

    return jax.shard_map(local_step, mesh=mesh, in_specs=(P('dp', None), P('dp'), P('dp'), P('dp'), P('dp'), P()),
                         out_specs=(P(), P('dp'), P('dp'), P('dp'), P()), check_vma=False)
```

time: 1290 us -> 230 us (0.18)
  other arithmetic: 636 us -> 0 us
  blocking collectives: 381 us -> 0 us
  Pallas kernels: 0 us -> 208 us
  waiting for transfers between devices: 177 us -> 0 us
  local copies, waits for them, and re-layouts: 82.1 us -> 14.9 us
  between operations: 16.6 us -> 2.49 us
    all_to_all x1 -> x0, blocking collectives: 341 us -> none  [local_step(): received = lax.all_to_all(grad_parts, 'dp', 0, 0, tiled=True)]
    all_to_all x1 -> x0, other arithmetic: 299 us -> none  [local_step(): received = lax.all_to_all(grad_parts, 'dp', 0, 0, tiled=True)]
    all_gather x1 -> x0, other arithmetic: 299 us -> none  [local_step(): params = lax.all_gather(new_master.astype(jnp.bfloat16), 'dp', tiled=True)]
    pallas_call x0 -> x1, Pallas kernels: none -> 208 us  [local_step(): pl.pallas_call(functools.partial(kernel, rows), out_shape=(jax.ShapeDtype...]
    all_gather x1 -> x0, waiting for transfers between devices: 177 us -> none  [local_step(): params = lax.all_gather(new_master.astype(jnp.bfloat16), 'dp', tiled=True)]
    unnamed x8 -> x12, local copies, waits for them, and re-layouts: 81.5 us -> 14.9 us
    psum x1 -> x0, blocking collectives: 39.5 us -> none  [local_step(): sq_total = lax.psum(jnp.sum(grad_mean * grad_mean), 'dp')]
    reduce_sum x2 -> x0, other arithmetic: 34.3 us -> none  [the longest x1 33.4 us: local_step(): grad_mean = jnp.sum(received, axis=0, dtype=jnp.float32) / num_dev]
  transfers between devices with their start and end apart: 1 -> 0, of which waited for: 1 -> 0; matrix products, arithmetic and copies ran while one was open for 0% -> 0% of each run, Pallas kernels for 0% -> 0%
where the time goes in v1:
time: 230 us; the launch traced here: 226 us
  Pallas kernels  208 us (90%)
  local copies, waits for them, and re-layouts  14.9 us (6%)
  between operations  2.49 us (1%)
    pallas_call x1, Pallas kernels, local_step(): pl.pallas_call(functools.partial(kernel, rows), out_shape=(jax.ShapeDtype...  208 us
    unnamed x12, local copies, waits for them, and re-layouts  14.9 us

profile of v1, /device:TPU:0, one launch (start us, length us, event | category | flops | bytes accessed | tf_op | source)
XLA Modules:
  0.0 225.5 jit_solution(15393439364301361103)
XLA Ops:
  1.3 208.1 %shard_map.101 = (bf16[29376,2,128]{2,1,0:T(2,128)(2,1)}, f32[1836,128]{1,0:T(8,128)}, f32[1836,128]{1,0:T(8,128)}, f32[1836,128]{1,0:T(8,128)}, f32[1,128]{1,0:T(1,128)}) custom-call(bf16[1,7520256]{1,0:T(2,128)(2,1)} %grad_hbm.1, f32[1836,128]{1,0:T(8,128)} %bitcast.14, f32[1836,128]{1,0:T(8,128)} %bitcast.15, f32[1836,128]{1,0:T(8,128)} %bitcast.16, ...), custom_call_target="tpu_custom_call" | custom-call | tf_op jit(solution)/shard_map/pallas_call | solution.py:383
  209.4 0.0 copy-start.2
  209.4 0.0 copy-start.1
  209.4 0.0 copy-start
  209.4 0.0 copy-start.3
  209.4 11.9 %copy.17 = bf16[7520256]{0:T(1024)(128)(2,1)} copy(bf16[7520256]{0:T(1024)(128)(2,1)} %bitcast.10) | data formatting | bytes 30081024
  221.4 0.0 copy-done.2
  221.4 1.0 copy.18
  222.4 0.0 copy-done.1
  222.4 1.0 copy.19
  223.4 0.0 copy-done
  223.4 1.0 copy.20
  224.4 0.0 copy-done.3
Async XLA Ops:
  209.4 12.0 %copy-start.2 = (f32[1836,128]{1,0:T(8,128)S(1)}, f32[1836,128]{1,0:T(8,128)}, u32[]{:S(2)}) copy-start(f32[1836,128]{1,0:T(8,128)} %get-tuple-element.11) | copy-start | bytes 2820100
  209.4 13.0 %copy-start.1 = (f32[1836,128]{1,0:T(8,128)S(1)}, f32[1836,128]{1,0:T(8,128)}, u32[]{:S(2)}) copy-start(f32[1836,128]{1,0:T(8,128)} %get-tuple-element.12) | copy-start | bytes 2820100
  209.4 14.0 %copy-start = (f32[1836,128]{1,0:T(8,128)S(1)}, f32[1836,128]{1,0:T(8,128)}, u32[]{:S(2)}) copy-start(f32[1836,128]{1,0:T(8,128)} %get-tuple-element.13) | copy-start | bytes 2820100
  209.4 14.9 %copy-start.3 = (f32[1,128]{1,0:T(1,128)S(1)}, f32[1,128]{1,0:T(1,128)}, u32[]{:S(2)}) copy-start(f32[1,128]{1,0:T(1,128)} %get-tuple-element.14) | copy-start | bytes 1540

commit v2 on v0

v2 whole, which is shorter than its diff:
```python
import functools

import jax
import jax.numpy as jnp
from jax import lax
from jax.experimental import pallas as pl
from jax.experimental.pallas import tpu as pltpu
from jax.sharding import PartitionSpec as P

BETA_FIRST = 0.9
BETA_SECOND = 0.95
ADAM_EPS = 1e-8
CLIP_EPS = 1e-6
WEIGHT_DECAY = 0.1
ADAM_STEP = 10
LANES = 128
TILE = 16
STAGES = 6
SHARE = 0.386
VMEM_LIMIT = 46 * 1024 * 1024
MESH = pl.DeviceIdType.MESH
F32 = jnp.float32
BF16 = jnp.bfloat16

HIGH, LOW, Y, X, CORE = range(5)
COLOURS = ((X, Y, LOW, HIGH), (Y, X, LOW, HIGH), (LOW, HIGH, X, Y))
GROUPS = ((1, 1), (0, 1), (1, 0), (0, 0))
HALF = ((1, 1), (1, 0), (0, 1), (0, 0))


def parts_of(rows):
    near = max(1, int((rows // TILE) * SHARE)) * TILE
    return (near, near, rows - 2 * near)


def padded(n):
    return -(-n // 8) * 8


def over_rows(rows, group, body):
    size = group * TILE
    whole = rows // size

    def step(i, carry):
        body(pl.multiple_of(i * size, size), size)
        return carry

    if whole:
        lax.fori_loop(0, whole, step, 0)
    at = whole * size
    if rows - at >= TILE:
        body(at, (rows - at) // TILE * TILE)
        at += (rows - at) // TILE * TILE
    if rows > at:
        body(at, rows - at)


def half_of(at):
    return at // 2 if isinstance(at, int) else lax.div(at, 2)


def kernel(rows, grad_hbm, w_hbm, m_hbm, v_hbm, d_hbm, lr_ref, full, w, m, v, norm_ref, *scratch):
    stages = scratch[:STAGES]
    scratch = scratch[STAGES:]
    got1, kept, sent2, got2, got3 = (scratch[3 * i:3 * i + 3] for i in range(5))
    (d, partial, stage_sem, state_sem, s1, r1, s2, r2, s3, r3, ns, nr,
     gs1, gr1, gs2, gr2, gs3, gr3, gs4, gr4) = scratch[15:]
    colours = range(3)
    part = parts_of(rows)
    first = (0, part[0], part[0] + part[1])
    units = rows // 2

    me = lax.axis_index('dp')
    bits = (lax.div(me, 16), lax.rem(lax.div(me, 8), 2), lax.rem(lax.div(me, 4), 2), lax.rem(lax.div(me, 2), 2),
            lax.rem(me, 2))

    def across(*flips):
        total = 0
        for bit in range(5):
            value = 1 - bits[bit] if bit in flips else bits[bit]
            total = total * 2 + value
        return total

    def pick(axes, values):
        return tuple(a for a, val in zip(axes, values) if val)

    def where(col, g, j2, j1, jc):
        d1, d2, d3, d4 = COLOURS[col]
        return pick((d1, d2, d3, d4, CORE), (j1, j2) + GROUPS[g] + (jc,))

    def piece(ref, k, col):
        return ref.at[pl.ds(k * units + first[col] // 2, part[col] // 2)]

    def send(src, dst, send_sem, recv_sem, flips):
        return pltpu.make_async_remote_copy(
            src_ref=src, dst_ref=dst, send_sem=send_sem, recv_sem=recv_sem,
            device_id=(across(*flips),), device_id_type=MESH)

    def state_copy(i):
        return pltpu.make_async_copy((w_hbm, m_hbm, v_hbm, d_hbm)[i], (w, m, v, d)[i], state_sem.at[i])

    work = [(g, j2, j1, jc, col) for g in range(4) for j2 in (1, 0) for j1, jc in HALF for col in colours]

    def stage_copy(i):
        g, j2, j1, jc, col = work[i]
        k = across(*where(col, g, j2, j1, jc))
        at = pl.multiple_of((k * rows + first[col]) * LANES, LANES)
        return pltpu.make_async_copy(grad_hbm.at[:, pl.ds(at, part[col] * LANES)],
                                     stages[i % STAGES].at[:, pl.ds(0, part[col] * LANES)], stage_sem.at[i % STAGES])

    def first_copy(col, g, j2, slot):
        j1 = 1 if slot else 0
        jc = 0 if slot == 1 else 1
        d1 = COLOURS[col][0]
        return send(piece(full, across(*where(col, g, j2, j1, jc)), col), got1[col].at[g, j2, slot],
                    s1.at[col, g, j2, slot], r1.at[col, g, j2, slot], pick((d1, CORE), (j1, jc)))

    def second_copy(col, g):
        return send(sent2[col].at[g], got2[col].at[g], s2.at[col, g], r2.at[col, g], (COLOURS[col][1],))

    def third_copy(col, g):
        return send(kept[col].at[g], got3[col].at[g], s3.at[col, g], r3.at[col, g], pick(COLOURS[col][2:], GROUPS[g]))

    def slot_of(j1, jc):
        return (2 if jc else 1) if j1 else 0

    def pack(i, start):
        g, j2, j1, jc, col = work[i]
        k = across(*where(col, g, j2, j1, jc))
        source = stages[i % STAGES]
        base = k * units + first[col] // 2
        stage_copy(i).wait()

        def body(at, size):
            lane = at * LANES
            if not isinstance(at, int):
                lane = pl.multiple_of(lane, TILE * LANES)
            val = source[:, pl.ds(lane, size * LANES)].astype(F32).reshape(size, LANES)
            full[pl.ds(base + half_of(at), size // 2)] = val.astype(BF16).reshape(size // 2, 2, LANES)

        over_rows(part[col], 4, body)
        if i + STAGES < len(work):
            stage_copy(i + STAGES).start()
        if start and (j1 or jc):
            first_copy(col, g, j2, slot_of(j1, jc)).start()

    def send_first(g, j2):
        for j1, jc in HALF[:3]:
            for col in colours:
                first_copy(col, g, j2, slot_of(j1, jc)).start()

    def four_sum(col, g, j2, target):
        for slot in (0, 1, 2):
            first_copy(col, g, j2, slot).wait_recv()
        base = across(*where(col, g, j2, 0, 0)) * units + first[col] // 2

        def body(at, size):
            near = pl.ds(half_of(at), size // 2)

            def wide(val):
                return val.reshape(size, LANES).astype(F32)

            mine = wide(full[pl.ds(base + half_of(at), size // 2)]) + wide(got1[col][g, j2, 0, near])
            other = wide(got1[col][g, j2, 1, near]) + wide(got1[col][g, j2, 2, near])
            target[g, pl.ds(at, size), :] = mine + other

        over_rows(part[col], 4, body)

    def plane_sum(col, g):
        def body(at, size):
            near = pl.ds(at, size)
            kept[col][g, near, :] = kept[col][g, near, :] + got2[col][g, near, :]

        over_rows(part[col], 4, body)

    everyone = [pick((HIGH, LOW, Y, X, CORE), [(n >> b) & 1 for b in (4, 3, 2, 1, 0)]) for n in range(1, 32)]

    for i in range(STAGES):
        stage_copy(i).start()
    barrier = pltpu.get_barrier_semaphore()
    for flips in everyone:
        pl.semaphore_signal(barrier, inc=1, device_id=(across(*flips),), device_id_type=MESH)
    size = len(work) // 4
    pack(0, False)
    pl.semaphore_wait(barrier, 31)
    first_copy(work[0][4], 0, 1, 2).start()
    for i in range(1, size):
        pack(i, True)
    for i in range(4):
        state_copy(i).start()
    for i in range(size, 2 * size):
        pack(i, False)

    for g in range(4):
        for col in colours:
            four_sum(col, g, 1, sent2[col])
        for col in colours:
            second_copy(col, g).start()
        if g < 3:
            send_first(g + 1, 1)
        for col in colours:
            four_sum(col, g, 0, kept[col])
        if g < 3:
            send_first(g + 1, 0)
        if g < 2:
            for i in range(size * (g + 2), size * (g + 3)):
                pack(i, False)
        for col in colours:
            second_copy(col, g).wait_recv()
            if g < 3:
                plane_sum(col, g)
        if g < 3:
            for col in colours:
                third_copy(col, g).start()

    for col in colours:
        for g in range(4):
            for j2 in (0, 1):
                for slot in range(3):
                    first_copy(col, g, j2, slot).wait_send()

    acc = jnp.zeros((8, LANES), F32)
    for col in colours:
        for g in range(3):
            third_copy(col, g).wait_recv()

        def mean_of(at, size):
            near = pl.ds(at, size)
            total = (kept[col][3, near, :] + got2[col][3, near, :]) + (got3[col][0, near, :] + got3[col][1, near, :])
            total = (total + got3[col][2, near, :]) * (1.0 / 32.0)
            kept[col][3, near, :] = total
            return total * total

        def fold(val):
            return jnp.sum(val.reshape(val.shape[0] // 8, 8, LANES), axis=0)

        whole = part[col] // 64
        if whole:
            acc = lax.fori_loop(0, whole, lambda i, a: a + fold(mean_of(pl.multiple_of(i * 64, 64), 64)), acc)
        at = whole * 64
        if part[col] - at >= 8:
            size = (part[col] - at) // 8 * 8
            acc = acc + fold(mean_of(at, size))
            at += size
        if part[col] > at:
            tail = mean_of(at, part[col] - at)
            acc = acc + jnp.concatenate([tail, jnp.zeros((8 - tail.shape[0], LANES), F32)], axis=0)

    partial[me] = acc

    def norm_copy(j, owner):
        return send(partial.at[owner], partial.at[owner], ns.at[j], nr.at[j], everyone[j])

    for j in range(31):
        norm_copy(j, me).start()
    for i in range(4):
        state_copy(i).wait()
    for j in range(31):
        norm_copy(j, across(*everyone[j])).wait_recv()
    norm = jnp.sqrt(jnp.full((1, LANES), jnp.sum(jnp.sum(partial[...], axis=0)), F32))
    norm_ref[...] = norm
    coef = jnp.minimum(1.0, 1.0 / (norm + CLIP_EPS))
    lr = lr_ref[0]

    def update(col):
        def body(at, size):
            near = pl.ds(first[col] + at, size)
            h = kept[col][3, pl.ds(at, size), :] * coef
            nm = BETA_FIRST * m[near, :] + (1.0 - BETA_FIRST) * h
            nv = BETA_SECOND * v[near, :] + (1.0 - BETA_SECOND) * h * h
            step = (nm * (1.0 / (1.0 - BETA_FIRST ** ADAM_STEP))) / (
                jnp.sqrt(nv * (1.0 / (1.0 - BETA_SECOND ** ADAM_STEP))) + ADAM_EPS)
            old = w[near, :]
            nw = old - lr * (step + WEIGHT_DECAY * d[near, :].astype(F32) * old)
            m[near, :] = nm
            v[near, :] = nv
            w[near, :] = nw
            full[pl.ds(me * units + first[col] // 2 + half_of(at), size // 2)] = nw.astype(BF16).reshape(
                size // 2, 2, LANES)

        over_rows(part[col], 2, body)

    def gather1(col, g):
        spot = piece(full, me, col)
        return send(spot, spot, gs1.at[col, g], gr1.at[col, g], pick(COLOURS[col][2:], GROUPS[g]))

    def gather1_in(col, g):
        spot = piece(full, across(*where(col, g, 0, 0, 0)), col)
        return send(spot, spot, gs1.at[col, g], gr1.at[col, g], pick(COLOURS[col][2:], GROUPS[g]))

    def gather2(col, g):
        spot = piece(full, across(*where(col, g, 0, 0, 0)), col)
        return send(spot, spot, gs2.at[col, g], gr2.at[col, g], (COLOURS[col][1],))

    def gather3(col, g, j2):
        spot = piece(full, across(*where(col, g, j2, 0, 0)), col)
        return send(spot, spot, gs3.at[col, g, j2], gr3.at[col, g, j2], (COLOURS[col][0],))

    def gather4(col, g, j2, j1):
        spot = piece(full, across(*where(col, g, j2, j1, 0)), col)
        return send(spot, spot, gs4.at[col, g, j2, j1], gr4.at[col, g, j2, j1], (CORE,))

    for col in (2, 0, 1):
        update(col)
        for g in (2, 1, 0):
            gather1(col, g).start()
        gather2(col, 3).start()
        gather3(col, 3, 0).start()
    for col in colours:
        gather4(col, 3, 0, 0).start()
    for g in (3, 2, 1, 0):
        if g < 3:
            for col in (2, 0, 1):
                gather1_in(col, g).wait_recv()
                gather2(col, g).start()
                gather3(col, g, 0).start()
                gather4(col, g, 0, 0).start()
        for col in (2, 0, 1):
            gather2(col, g).wait_recv()
            gather3(col, g, 1).start()
            gather4(col, g, 1, 0).start()
    for g in (3, 2, 1, 0):
        for j2 in (0, 1):
            for col in colours:
                gather3(col, g, j2).wait_recv()
                gather4(col, g, j2, 1).start()

    for col in colours:
        for g in (3, 2, 1, 0):
            for j2 in (0, 1):
                for j1 in (0, 1):
                    gather4(col, g, j2, j1).wait()
                gather3(col, g, j2).wait_send()
            gather2(col, g).wait_send()
            second_copy(col, g).wait_send()
        for g in range(3):
            gather1(col, g).wait_send()
            third_copy(col, g).wait_send()
    for j in range(31):
        norm_copy(j, me).wait_send()


def write_out(*refs):
    sem = refs[-1]
    count = len(refs) // 2
    copies = [pltpu.make_async_copy(refs[i], refs[count + i], sem.at[i]) for i in range(count)]
    for copy in copies:
        copy.start()
    for copy in copies:
        copy.wait()


def solution(mesh):
    num_dev = mesh.shape['dp']

    def local_step(grad_row, master, mom_first, mom_second, decay_mask, learn_rate):
        shard_len = master.shape[0]
        rows = shard_len // LANES
        part = parts_of(rows)
        dma = pltpu.SemaphoreType.DMA
        hbm = pl.BlockSpec(memory_space=pltpu.HBM)
        vmem = pl.BlockSpec(memory_space=pltpu.VMEM)
        flat = (rows, LANES)
        whole = (num_dev * rows // 2, 2, LANES)
        results = pl.pallas_call(
            functools.partial(kernel, rows),
            out_shape=(pltpu.VMEM(whole, BF16), pltpu.VMEM(flat, F32), pltpu.VMEM(flat, F32), pltpu.VMEM(flat, F32),
                       pltpu.VMEM((1, LANES), F32)),
            in_specs=[hbm] * 5 + [pl.BlockSpec(memory_space=pltpu.SMEM)],
            out_specs=(vmem,) * 5,
            scratch_shapes=[pltpu.VMEM((1, max(part) * LANES), BF16)] * STAGES
            + [pltpu.VMEM((4, 2, 3, n // 2, 2, LANES), BF16) for n in part]
            + [pltpu.VMEM((count, padded(n), LANES), F32) for count in (4, 4, 4, 3) for n in part]
            + [
                pltpu.VMEM(flat, jnp.int32), pltpu.VMEM((num_dev, 8, LANES), F32),
                dma((STAGES,)), dma((4,)),
                dma((3, 4, 2, 3)), dma((3, 4, 2, 3)), dma((3, 4)), dma((3, 4)), dma((3, 3)), dma((3, 3)),
                dma((num_dev - 1,)), dma((num_dev - 1,)),
                dma((3, 3)), dma((3, 3)), dma((3, 4)), dma((3, 4)), dma((3, 4, 2)), dma((3, 4, 2)),
                dma((3, 4, 2, 2)), dma((3, 4, 2, 2)),
            ],
            compiler_params=pltpu.CompilerParams(
                collective_id=0, has_side_effects=True, vmem_limit_bytes=VMEM_LIMIT),
        )(grad_row, master.reshape(flat), mom_first.reshape(flat), mom_second.reshape(flat), decay_mask.reshape(flat), learn_rate)
        state = jax.ShapeDtypeStruct(flat, F32)
        params, new_master, new_first, new_second, norm = pl.pallas_call(
            write_out,
            out_shape=(jax.ShapeDtypeStruct(whole, BF16), state, state, state, jax.ShapeDtypeStruct((1, LANES), F32)),
            in_specs=[vmem] * 5,
            out_specs=(hbm,) * 5,
            scratch_shapes=[dma((5,))],
            compiler_params=pltpu.CompilerParams(vmem_limit_bytes=1024 * 1024),
        )(*results)
        return (params.reshape(num_dev * shard_len), new_master.reshape(shard_len), new_first.reshape(shard_len),
                new_second.reshape(shard_len), norm[0, :1])

    return jax.shard_map(local_step, mesh=mesh, in_specs=(P('dp', None), P('dp'), P('dp'), P('dp'), P('dp'), P()),
                         out_specs=(P(), P('dp'), P('dp'), P('dp'), P()), check_vma=False)
```

time: 1290 us -> 230 us (0.18)
  other arithmetic: 636 us -> 0 us
  blocking collectives: 381 us -> 0 us
  Pallas kernels: 0 us -> 228 us
  waiting for transfers between devices: 177 us -> 0 us
  local copies, waits for them, and re-layouts: 82.1 us -> 0 us
  between operations: 16.6 us -> 1.29 us
    all_to_all x1 -> x0, blocking collectives: 341 us -> none  [local_step(): received = lax.all_to_all(grad_parts, 'dp', 0, 0, tiled=True)]
    all_to_all x1 -> x0, other arithmetic: 299 us -> none  [local_step(): received = lax.all_to_all(grad_parts, 'dp', 0, 0, tiled=True)]
    all_gather x1 -> x0, other arithmetic: 299 us -> none  [local_step(): params = lax.all_gather(new_master.astype(jnp.bfloat16), 'dp', tiled=True)]
    pallas_call x0 -> x2, Pallas kernels: none -> 228 us  [the longest x1 222 us: local_step(): pl.pallas_call(functools.partial(kernel, rows), out_shape=(pltpu.VMEM(who...]
    all_gather x1 -> x0, waiting for transfers between devices: 177 us -> none  [local_step(): params = lax.all_gather(new_master.astype(jnp.bfloat16), 'dp', tiled=True)]
    unnamed x8 -> x0, local copies, waits for them, and re-layouts: 81.5 us -> none
    psum x1 -> x0, blocking collectives: 39.5 us -> none  [local_step(): sq_total = lax.psum(jnp.sum(grad_mean * grad_mean), 'dp')]
    reduce_sum x2 -> x0, other arithmetic: 34.3 us -> none  [the longest x1 33.4 us: local_step(): grad_mean = jnp.sum(received, axis=0, dtype=jnp.float32) / num_dev]
  transfers between devices with their start and end apart: 1 -> 0, of which waited for: 1 -> 0; matrix products, arithmetic and copies ran while one was open for 0% -> 0% of each run, Pallas kernels for 0% -> 0%
where the time goes in v2:
time: 230 us; the launch traced here: 229 us
  Pallas kernels  228 us (99%)
    pallas_call x1, Pallas kernels, local_step(): pl.pallas_call(functools.partial(kernel, rows), out_shape=(pltpu.VMEM(who...  222 us
    pallas_call x1, Pallas kernels, local_step(): pl.pallas_call(write_out, out_shape=(jax.ShapeDtypeStruct(whole, BF16), s...  6.49 us

profile of v2, /device:TPU:0, one launch (start us, length us, event | category | flops | bytes accessed | tf_op | source)
XLA Modules:
  0.0 229.3 jit_solution(3421504432614960698)
XLA Ops:
  1.3 221.5 %shard_map.101 = (bf16[29376,2,128]{2,1,0:T(2,128)(2,1)S(1)}, f32[1836,128]{1,0:T(8,128)S(1)}, f32[1836,128]{1,0:T(8,128)S(1)}, f32[1836,128]{1,0:T(8,128)S(1)}, f32[1,128]{1,0:T(1,128)S(1)}) custom-call(bf16[1,7520256]{1,0:T(2,128)(2,1)} %grad_hbm.1, f32[1836,128]{1,0:T(8,128)} %bitcast.10, f32[1836,128]{1,0:T(8,128)} %bitcast.11, f32[1836,128]{1,0:T(8,128)} %bitcast.12, ...), custom_call_target="tpu_custom_call" | custom-call | tf_op jit(solution)/shard_map/pallas_call | solution.py:365
  222.8 6.5 %shard_map.102 = (bf16[29376,2,128]{2,1,0:T(2,128)(2,1)}, f32[1836,128]{1,0:T(8,128)}, f32[1836,128]{1,0:T(8,128)}, f32[1836,128]{1,0:T(8,128)}, f32[1,128]{1,0:T(1,128)}) custom-call(bf16[29376,2,128]{2,1,0:T(2,128)(2,1)S(1)} %get-tuple-element.15.refs_0_, f32[1836,128]{1,0:T(8,128)S(1)} %get-tuple-element.16.refs_1_, ...), custom_call_target="tpu_custom_call" | custom-call | tf_op jit(solution)/shard_map/pallas_call | solution.py:386

commit v3 on v0

v3 whole, which is shorter than its diff:
```python
import functools

import jax
import jax.numpy as jnp
from jax import lax
from jax.experimental import pallas as pl
from jax.experimental.pallas import tpu as pltpu
from jax.sharding import PartitionSpec as P

BETA_FIRST = 0.9
BETA_SECOND = 0.95
ADAM_EPS = 1e-8
CLIP_EPS = 1e-6
WEIGHT_DECAY = 0.1
ADAM_STEP = 10
LANES = 128
TILE = 16
STAGES = 4
VMEM_LIMIT = 46 * 1024 * 1024
MESH = pl.DeviceIdType.MESH
F32 = jnp.float32
BF16 = jnp.bfloat16

HIGH, LOW, Y, X, CORE = range(5)
REDUCE = (
    ((X, Y, LOW, HIGH), ((1, 1), (1, 0), (0, 1), (0, 0))),
    ((Y, X, LOW, HIGH), ((1, 1), (1, 0), (0, 1), (0, 0))),
    ((LOW, HIGH, X, Y), ((1, 1), (1, 0), (0, 1), (0, 0))),
)
REDUCE_TILES = (47, 47, 20)
SPAN_OF = (0, 0, 1)
GATHER = (
    ((X, Y, LOW, HIGH), ((0, 1), (1, 0), (1, 1), (0, 0))),
    ((Y, X, LOW, HIGH), ((0, 1), (1, 0), (1, 1), (0, 0))),
    ((LOW, HIGH, X, Y), ((0, 1), (1, 0), (1, 1), (0, 0))),
)
GATHER_TILES = (48, 48, 18)
REDUCE_ORDER = (
    (0, 1, 0, 1, 1, 1), (1, 2, 0, 1, 2, -1), (0, 0, 0, 1, 1, 1), (1, 0, 0, 1, 2, -1), (1, 1, 0, 1, 2, -1),
    (0, 1, 0, 1, 1, 0), (1, 2, 0, 1, 1, -1), (0, 0, 0, 1, 1, 0), (1, 0, 0, 1, 1, -1), (1, 1, 0, 1, 1, -1),
    (0, 1, 0, 1, 0, 1), (1, 2, 0, 1, 0, -1), (0, 0, 0, 1, 0, 1), (1, 0, 0, 1, 0, -1), (1, 1, 0, 0, 2, -1),
    (0, 1, 0, 1, 0, 0), (0, 0, 0, 1, 0, 0), (1, 1, 0, 0, 1, -1), (0, 1, 0, 0, 1, 1), (1, 2, 0, 0, 2, -1),
    (0, 0, 0, 0, 1, 1), (1, 1, 0, 1, 0, -1), (1, 0, 0, 0, 2, -1), (0, 1, 0, 0, 1, 0), (1, 2, 0, 0, 1, -1),
    (0, 0, 0, 0, 1, 0), (1, 0, 0, 0, 1, -1), (0, 1, 0, 0, 0, 1), (1, 2, 0, 0, 0, -1), (0, 0, 0, 0, 0, 1),
    (1, 0, 0, 0, 0, -1), (1, 1, 0, 0, 0, -1), (0, 1, 0, 0, 0, 0), (0, 0, 0, 0, 0, 0), (0, 1, 1, 1, 1, 1),
    (1, 2, 1, 1, 2, -1), (0, 0, 1, 1, 1, 1), (0, 1, 1, 1, 1, 0), (1, 2, 1, 1, 1, -1), (0, 0, 1, 1, 1, 0),
    (0, 1, 1, 1, 0, 1), (1, 2, 1, 1, 0, -1), (0, 0, 1, 1, 0, 1), (0, 1, 1, 1, 0, 0), (0, 0, 1, 1, 0, 0), (2, 2, 0),
    (0, 1, 1, 0, 1, 1), (1, 2, 1, 0, 2, 0), (0, 0, 1, 0, 1, 1), (0, 1, 1, 0, 1, 0), (1, 2, 1, 0, 1, 0),
    (0, 0, 1, 0, 1, 0), (0, 1, 1, 0, 0, 1), (1, 2, 1, 0, 0, 0), (0, 0, 1, 0, 0, 1), (0, 1, 1, 0, 0, 0),
    (0, 0, 1, 0, 0, 0), (0, 1, 2, 1, 1, 1), (0, 0, 2, 1, 1, 1), (0, 1, 2, 1, 1, 0), (0, 0, 2, 1, 1, 0),
    (0, 1, 2, 1, 0, 1), (0, 0, 2, 1, 0, 1), (0, 1, 2, 1, 0, 0), (0, 0, 2, 1, 0, 0), (0, 1, 2, 0, 1, 1),
    (0, 0, 2, 0, 1, 1), (0, 1, 2, 0, 1, 0), (0, 0, 2, 0, 1, 0), (2, 0, 0), (2, 1, 0), (3, 2, 0), (1, 0, 1, 1, 2, 0),
    (1, 1, 1, 1, 2, 0), (0, 1, 2, 0, 0, 1), (1, 0, 1, 1, 1, 0), (1, 1, 1, 1, 1, 0), (1, 0, 1, 1, 0, 0),
    (1, 1, 1, 1, 0, 0), (1, 2, 2, 1, 2, 1), (1, 2, 2, 1, 1, 1), (1, 2, 2, 1, 0, 1), (0, 0, 2, 0, 0, 1),
    (0, 1, 2, 0, 0, 0), (0, 0, 2, 0, 0, 0), (0, 1, 3, 1, 1, 1), (0, 0, 3, 1, 1, 1), (0, 1, 3, 1, 1, 0),
    (0, 0, 3, 1, 1, 0), (0, 1, 3, 1, 0, 1), (0, 0, 3, 1, 0, 1), (0, 1, 3, 1, 0, 0), (0, 0, 3, 1, 0, 0),
    (0, 1, 3, 0, 1, 1), (0, 0, 3, 0, 1, 1), (0, 1, 3, 0, 1, 0), (0, 0, 3, 0, 1, 0), (0, 1, 3, 0, 0, 1),
    (0, 0, 3, 0, 0, 1), (0, 1, 3, 0, 0, 0), (0, 0, 3, 0, 0, 0), (2, 2, 1), (1, 2, 2, 0, 2, 2), (1, 2, 2, 0, 1, 2),
    (1, 2, 2, 0, 0, 2), (3, 0, 0), (3, 1, 0), (1, 0, 1, 0, 2, 1), (1, 1, 1, 0, 2, 1), (1, 0, 1, 0, 1, 1),
    (1, 1, 1, 0, 1, 1), (1, 0, 1, 0, 0, 1), (1, 1, 1, 0, 0, 1), (4, 2, 0), (3, 2, 1), (1, 2, 3, 1, 2, 3),
    (1, 2, 3, 1, 1, 3), (1, 2, 3, 1, 0, 3), (4, 1, 0), (4, 0, 0), (2, 2, 2), (1, 2, 3, 0, 2, 4), (1, 2, 3, 0, 1, 4),
    (1, 2, 3, 0, 0, 4), (4, 2, 1), (2, 0, 1), (2, 1, 1), (1, 0, 2, 1, 2, 2), (1, 1, 2, 1, 2, 2), (1, 0, 2, 1, 1, 2),
    (1, 1, 2, 1, 1, 2), (1, 0, 2, 1, 0, 2), (1, 1, 2, 1, 0, 2), (3, 2, 2), (2, 2, 3), (3, 0, 1), (1, 0, 2, 0, 2, 3),
    (1, 0, 2, 0, 1, 3), (1, 0, 2, 0, 0, 3), (3, 1, 1), (1, 1, 2, 0, 2, 3), (1, 1, 2, 0, 1, 3), (1, 1, 2, 0, 0, 3),
    (4, 1, 1), (4, 0, 1), (2, 0, 2), (2, 1, 2), (1, 0, 3, 1, 2, 4), (1, 1, 3, 1, 2, 4), (1, 0, 3, 1, 1, 4),
    (1, 1, 3, 1, 1, 4), (1, 0, 3, 1, 0, 4), (1, 1, 3, 1, 0, 4), (3, 0, 2), (3, 1, 2), (1, 0, 3, 0, 2, 5),
    (1, 1, 3, 0, 2, 5), (1, 0, 3, 0, 1, 5), (1, 1, 3, 0, 1, 5), (1, 0, 3, 0, 0, 5), (1, 1, 3, 0, 0, 5), (4, 2, 2),
    (4, 1, 2), (3, 2, 3), (4, 0, 2), (4, 2, 3), (2, 0, 3), (2, 1, 3), (3, 0, 3), (5, 2, 0), (3, 1, 3), (4, 1, 3),
    (4, 0, 3), (5, 1, 0), (5, 0, 0),
)
GATHER_ORDER = (
    (0, 0, 0, 0), (0, 1, 0, 0), (0, 2, 0, 0), (1, 0, 0, 0), (1, 1, 0, 0), (1, 2, 0, 0), (2, 0, 0, 0), (2, 1, 0, 0),
    (2, 2, 0, 0), (5, 0, 3, 0), (4, 0, 3, 0), (4, 1, 3, 0), (5, 1, 3, 0), (3, 0, 2, 0), (3, 2, 1, 0), (3, 2, 2, 0),
    (3, 0, 1, 0), (3, 2, 0, 0), (5, 0, 3, 1), (3, 0, 0, 0), (5, 1, 3, 1), (5, 0, 1, 0), (5, 0, 2, 0), (4, 0, 1, 0),
    (4, 0, 2, 0), (3, 1, 2, 0), (5, 0, 0, 0), (3, 1, 1, 0), (4, 0, 0, 0), (5, 1, 1, 0), (5, 0, 1, 1), (5, 0, 2, 1),
    (5, 1, 2, 0), (3, 1, 0, 0), (4, 2, 3, 0), (4, 1, 2, 0), (5, 2, 3, 0), (4, 2, 1, 0), (5, 1, 0, 0), (5, 2, 1, 0),
    (4, 1, 1, 0), (5, 1, 2, 1), (4, 2, 2, 0), (5, 2, 2, 0), (4, 1, 0, 0), (5, 0, 0, 1), (4, 2, 0, 0), (5, 1, 1, 1),
    (5, 2, 0, 0), (5, 2, 3, 1), (5, 2, 1, 1), (5, 1, 0, 1), (5, 2, 2, 1), (5, 2, 0, 1),
)
HALF = ((1, 1), (1, 0), (0, 1), (0, 0))


def parts_of(rows, tiles):
    full = rows // TILE
    part = [max(1, full * n // sum(tiles)) * TILE for n in tiles[:-1]]
    return part + [rows - sum(part)]


def padded(n, unit):
    return -(-n // unit) * unit


def over_rows(rows, group, body):
    size = group * TILE
    whole = rows // size

    def step(i, carry):
        body(pl.multiple_of(i * size, size), size)
        return carry

    if whole:
        lax.fori_loop(0, whole, step, 0)
    at = whole * size
    if rows - at >= TILE:
        body(at, (rows - at) // TILE * TILE)
        at += (rows - at) // TILE * TILE
    if rows > at:
        body(at, rows - at)


def half_of(at):
    return at // 2 if isinstance(at, int) else lax.div(at, 2)


def kernel(rows, grad_hbm, w_hbm, m_hbm, v_hbm, d_hbm, lr_ref, full, w, m, v, norm_ref, *scratch):
    count = len(REDUCE)
    stages = scratch[:STAGES]
    scratch = scratch[STAGES:]
    got1, kept, sent2, got2, got3 = (scratch[count * i:count * i + count] for i in range(5))
    (row, mean, d, partial, stage_sem, state_sem, s1, r1, s2, r2, s3, r3, ns, nr,
     gs1, gr1, gs2, gr2, gs3, gr3, gs4, gr4) = scratch[5 * count:]
    part = parts_of(rows, REDUCE_TILES)
    first = [sum(part[:i]) for i in range(count)]
    units = rows // 2
    gather_part = parts_of(rows, GATHER_TILES)
    gather_first = [sum(gather_part[:i]) for i in range(len(gather_part))]

    me = lax.axis_index('dp')
    bits = (lax.div(me, 16), lax.rem(lax.div(me, 8), 2), lax.rem(lax.div(me, 4), 2), lax.rem(lax.div(me, 2), 2),
            lax.rem(me, 2))

    def across(*flips):
        total = 0
        for bit in range(5):
            value = 1 - bits[bit] if bit in flips else bits[bit]
            total = total * 2 + value
        return total

    def pick(axes, values):
        return tuple(a for a, val in zip(axes, values) if val)

    def where(colour, g, j2, j1, jc):
        axes, groups = colour
        return pick(axes + (CORE,), (j1, j2) + groups[g] + (jc,))

    def send(src, dst, send_sem, recv_sem, flips):
        return pltpu.make_async_remote_copy(
            src_ref=src, dst_ref=dst, send_sem=send_sem, recv_sem=recv_sem,
            device_id=(across(*flips),), device_id_type=MESH)

    waited = set()

    def need(copy_of, *key):
        if (copy_of.__name__,) + key not in waited:
            waited.add((copy_of.__name__,) + key)
            copy_of(*key).wait_recv()

    def state_copy(i):
        return pltpu.make_async_copy((w_hbm, m_hbm, v_hbm, d_hbm)[i], (w, m, v, d)[i], state_sem.at[i])

    work = [task[1:] for task in REDUCE_ORDER if task[0] == 0]
    spans = []
    for lead in range(2):
        inside = [i for i in range(count) if SPAN_OF[i] == lead]
        spans.append((inside[0], first[inside[0]], sum(part[i] for i in inside)))

    def stage_copy(i):
        span, g, j2, j1, jc = work[i]
        c, begin, length = spans[span]
        k = across(*where(REDUCE[c], g, j2, j1, jc))
        at = pl.multiple_of((k * rows + begin) * LANES, LANES)
        return pltpu.make_async_copy(grad_hbm.at[:, pl.ds(at, length * LANES)],
                                     stages[i % STAGES].at[:, pl.ds(0, length * LANES)], stage_sem.at[i % STAGES])

    def first_copy(c, g, j2, slot):
        j1 = 1 if slot else 0
        jc = 0 if slot == 1 else 1
        k = across(*where(REDUCE[c], g, j2, j1, jc))
        return send(row.at[k, pl.ds(first[c], padded(part[c], TILE))], got1[c].at[g, j2, slot],
                    s1.at[c, g, j2, slot], r1.at[c, g, j2, slot], pick((REDUCE[c][0][0], CORE), (j1, jc)))

    def second_copy(c, g):
        return send(sent2[c].at[g], got2[c].at[g], s2.at[c, g], r2.at[c, g], (REDUCE[c][0][1],))

    def third_copy(c, g):
        return send(kept[c].at[g], got3[c].at[g], s3.at[c, g], r3.at[c, g], pick(REDUCE[c][0][2:], REDUCE[c][1][g]))

    def pack(i):
        span, g, j2, j1, jc = work[i]
        c, begin, length = spans[span]
        k = across(*where(REDUCE[c], g, j2, j1, jc))
        source = stages[i % STAGES]
        stage_copy(i).wait()

        def body(at, size):
            lane = at * LANES
            if not isinstance(at, int):
                lane = pl.multiple_of(lane, TILE * LANES)
            val = source[:, pl.ds(lane, size * LANES)].astype(F32).reshape(size, LANES)
            row[k, pl.ds(begin + at, size), :] = val.astype(BF16)

        over_rows(length, 4, body)
        if i + STAGES < len(work):
            stage_copy(i + STAGES).start()

    def four_sum(c, g, j2, target):
        for slot in (0, 1, 2):
            need(first_copy, c, g, j2, slot)
        k = across(*where(REDUCE[c], g, j2, 0, 0))

        def body(at, size):
            near = pl.ds(at, size)
            mine = row[k, pl.ds(first[c] + at, size), :].astype(F32) + got1[c][g, j2, 0, near, :].astype(F32)
            other = got1[c][g, j2, 1, near, :].astype(F32) + got1[c][g, j2, 2, near, :].astype(F32)
            target[g, near, :] = mine + other

        over_rows(part[c], 4, body)

    def plane_sum(c, g):
        need(second_copy, c, g)

        def body(at, size):
            near = pl.ds(at, size)
            kept[c][g, near, :] = kept[c][g, near, :] + got2[c][g, near, :]

        if g < 3:
            over_rows(part[c], 4, body)
            third_copy(c, g).start()

    def final(c, acc):
        for g in range(3):
            need(third_copy, c, g)

        def mean_of(at, size):
            near = pl.ds(at, size)
            total = (kept[c][3, near, :] + got2[c][3, near, :]) + (got3[c][0, near, :] + got3[c][1, near, :])
            total = (total + got3[c][2, near, :]) * (1.0 / 32.0)
            mean[pl.ds(first[c] + at, size), :] = total
            return total * total

        def fold(val):
            return jnp.sum(val.reshape(val.shape[0] // 8, 8, LANES), axis=0)

        whole = part[c] // 64
        if whole:
            acc = lax.fori_loop(0, whole, lambda i, a: a + fold(mean_of(pl.multiple_of(i * 64, 64), 64)), acc)
        at = whole * 64
        if part[c] - at >= 8:
            size = (part[c] - at) // 8 * 8
            acc = acc + fold(mean_of(at, size))
            at += size
        if part[c] > at:
            tail = mean_of(at, part[c] - at)
            acc = acc + jnp.concatenate([tail, jnp.zeros((8 - tail.shape[0], LANES), F32)], axis=0)
        return acc

    everyone = [pick((HIGH, LOW, Y, X, CORE), [(n >> b) & 1 for b in (4, 3, 2, 1, 0)]) for n in range(1, 32)]

    for i in range(STAGES):
        stage_copy(i).start()
    barrier = pltpu.get_barrier_semaphore()
    for flips in everyone:
        pl.semaphore_signal(barrier, inc=1, device_id=(across(*flips),), device_id_type=MESH)

    acc = jnp.zeros((8, LANES), F32)
    packed = 0
    entered = False
    for task in REDUCE_ORDER:
        kind, c, g = task[:3]
        if kind == 0:
            pack(packed)
            packed += 1
            if packed == len(work):
                for i in range(4):
                    state_copy(i).start()
        elif kind == 1:
            if not entered:
                pl.semaphore_wait(barrier, 31)
                entered = True
            j2, slot, h = task[3:]
            if h >= 0:
                for other in range(3):
                    need(first_copy, c, h // 2, 1 - h % 2, other)
            first_copy(c, g, j2, slot).start()
        elif kind == 2:
            four_sum(c, g, 1, sent2[c])
            second_copy(c, g).start()
        elif kind == 3:
            four_sum(c, g, 0, kept[c])
        elif kind == 4:
            plane_sum(c, g)
        else:
            acc = final(c, acc)

    partial[me] = acc

    def norm_copy(j, owner):
        return send(partial.at[owner], partial.at[owner], ns.at[j], nr.at[j], everyone[j])

    for j in range(31):
        norm_copy(j, me).start()
    for i in range(4):
        state_copy(i).wait()
    for j in range(31):
        norm_copy(j, across(*everyone[j])).wait_recv()
    norm = jnp.sqrt(jnp.full((1, LANES), jnp.sum(jnp.sum(partial[...], axis=0)), F32))
    norm_ref[...] = norm
    coef = jnp.minimum(1.0, 1.0 / (norm + CLIP_EPS))
    lr = lr_ref[0]

    def update(c):
        def body(at, size):
            near = pl.ds(gather_first[c] + at, size)
            h = mean[near, :] * coef
            nm = BETA_FIRST * m[near, :] + (1.0 - BETA_FIRST) * h
            nv = BETA_SECOND * v[near, :] + (1.0 - BETA_SECOND) * h * h
            step = (nm * (1.0 / (1.0 - BETA_FIRST ** ADAM_STEP))) / (
                jnp.sqrt(nv * (1.0 / (1.0 - BETA_SECOND ** ADAM_STEP))) + ADAM_EPS)
            old = w[near, :]
            nw = old - lr * (step + WEIGHT_DECAY * d[near, :].astype(F32) * old)
            m[near, :] = nm
            v[near, :] = nv
            w[near, :] = nw
            full[pl.ds(me * units + gather_first[c] // 2 + half_of(at), size // 2)] = nw.astype(BF16).reshape(
                size // 2, 2, LANES)

        over_rows(gather_part[c], 2, body)

    def piece(c, g, j2, j1):
        k = across(*where(GATHER[c], g, j2, j1, 0))
        return full.at[pl.ds(k * units + gather_first[c] // 2, gather_part[c] // 2)]

    def gather1(c, g):
        spot = piece(c, 3, 0, 0)
        return send(spot, spot, gs1.at[c, g], gr1.at[c, g], pick(GATHER[c][0][2:], GATHER[c][1][g]))

    def gather1_in(c, g):
        spot = piece(c, g, 0, 0)
        return send(spot, spot, gs1.at[c, g], gr1.at[c, g], pick(GATHER[c][0][2:], GATHER[c][1][g]))

    def gather2(c, g):
        spot = piece(c, g, 0, 0)
        return send(spot, spot, gs2.at[c, g], gr2.at[c, g], (GATHER[c][0][1],))

    def gather3(c, g, j2):
        spot = piece(c, g, j2, 0)
        return send(spot, spot, gs3.at[c, g, j2], gr3.at[c, g, j2], (GATHER[c][0][0],))

    def gather4(c, g, j2, j1):
        spot = piece(c, g, j2, j1)
        return send(spot, spot, gs4.at[c, g, j2, j1], gr4.at[c, g, j2, j1], (CORE,))

    for kind, c, g, j2 in GATHER_ORDER:
        if kind == 0:
            update(c)
        elif kind == 1:
            for group in (2, 1, 0):
                gather1(c, group).start()
            gather2(c, 3).start()
            gather3(c, 3, 0).start()
        elif kind == 2:
            gather4(c, 3, 0, 0).start()
        elif kind == 3:
            gather1_in(c, g).wait_recv()
            gather2(c, g).start()
            gather3(c, g, 0).start()
            gather4(c, g, 0, 0).start()
        elif kind == 4:
            gather2(c, g).wait_recv()
            gather3(c, g, 1).start()
            gather4(c, g, 1, 0).start()
        else:
            gather3(c, g, j2).wait_recv()
            gather4(c, g, j2, 1).start()

    for c in range(count):
        for g in range(4):
            for j2 in (0, 1):
                for slot in range(3):
                    first_copy(c, g, j2, slot).wait_send()
            second_copy(c, g).wait_send()
        for g in range(3):
            third_copy(c, g).wait_send()
    for j in range(31):
        norm_copy(j, me).wait_send()
    for c in range(len(GATHER)):
        for g in range(3):
            gather1(c, g).wait_send()
        for g in range(4):
            gather2(c, g).wait_send()
            for j2 in (0, 1):
                gather3(c, g, j2).wait_send()
                for j1 in (0, 1):
                    gather4(c, g, j2, j1).wait()


def write_out(*refs):
    sem = refs[-1]
    count = len(refs) // 2
    copies = [pltpu.make_async_copy(refs[i], refs[count + i], sem.at[i]) for i in range(count)]
    for copy in copies:
        copy.start()
    for copy in copies:
        copy.wait()


def solution(mesh):
    num_dev = mesh.shape['dp']

    def local_step(grad_row, master, mom_first, mom_second, decay_mask, learn_rate):
        shard_len = master.shape[0]
        rows = shard_len // LANES
        part = parts_of(rows, REDUCE_TILES)
        dma = pltpu.SemaphoreType.DMA
        hbm = pl.BlockSpec(memory_space=pltpu.HBM)
        vmem = pl.BlockSpec(memory_space=pltpu.VMEM)
        flat = (rows, LANES)
        whole = (num_dev * rows // 2, 2, LANES)
        n = len(REDUCE)
        longest = max(sum(part[i] for i in range(n) if SPAN_OF[i] == lead) for lead in range(2))
        k = len(GATHER)
        results = pl.pallas_call(
            functools.partial(kernel, rows),
            out_shape=(pltpu.VMEM(whole, BF16), pltpu.VMEM(flat, F32), pltpu.VMEM(flat, F32), pltpu.VMEM(flat, F32),
                       pltpu.VMEM((1, LANES), F32)),
            in_specs=[hbm] * 5 + [pl.BlockSpec(memory_space=pltpu.SMEM)],
            out_specs=(vmem,) * 5,
            scratch_shapes=[pltpu.VMEM((1, longest * LANES), BF16)] * STAGES
            + [pltpu.VMEM((4, 2, 3, padded(p, TILE), LANES), BF16) for p in part]
            + [pltpu.VMEM((groups, padded(p, 8), LANES), F32) for groups in (4, 4, 4, 3) for p in part]
            + [
                pltpu.VMEM((num_dev, padded(rows, TILE), LANES), BF16), pltpu.VMEM(flat, F32),
                pltpu.VMEM(flat, jnp.int32), pltpu.VMEM((num_dev, 8, LANES), F32),
                dma((STAGES,)), dma((4,)),
                dma((n, 4, 2, 3)), dma((n, 4, 2, 3)), dma((n, 4)), dma((n, 4)), dma((n, 3)), dma((n, 3)),
                dma((num_dev - 1,)), dma((num_dev - 1,)),
                dma((k, 3)), dma((k, 3)), dma((k, 4)), dma((k, 4)), dma((k, 4, 2)), dma((k, 4, 2)),
                dma((k, 4, 2, 2)), dma((k, 4, 2, 2)),
            ],
            compiler_params=pltpu.CompilerParams(
                collective_id=0, has_side_effects=True, vmem_limit_bytes=VMEM_LIMIT),
        )(grad_row, master.reshape(flat), mom_first.reshape(flat), mom_second.reshape(flat), decay_mask.reshape(flat), learn_rate)
        state = jax.ShapeDtypeStruct(flat, F32)
        params, new_master, new_first, new_second, norm = pl.pallas_call(
            write_out,
            out_shape=(jax.ShapeDtypeStruct(whole, BF16), state, state, state, jax.ShapeDtypeStruct((1, LANES), F32)),
            in_specs=[vmem] * 5,
            out_specs=(hbm,) * 5,
            scratch_shapes=[dma((5,))],
            compiler_params=pltpu.CompilerParams(vmem_limit_bytes=1024 * 1024),
        )(*results)
        return (params.reshape(num_dev * shard_len), new_master.reshape(shard_len), new_first.reshape(shard_len),
                new_second.reshape(shard_len), norm[0, :1])

    return jax.shard_map(local_step, mesh=mesh, in_specs=(P('dp', None), P('dp'), P('dp'), P('dp'), P('dp'), P()),
                         out_specs=(P(), P('dp'), P('dp'), P('dp'), P()), check_vma=False)
```

time: 1290 us -> 208 us (0.16)
  other arithmetic: 636 us -> 0 us
  blocking collectives: 381 us -> 0 us
  Pallas kernels: 0 us -> 207 us
  waiting for transfers between devices: 177 us -> 0 us
  local copies, waits for them, and re-layouts: 82.1 us -> 0 us
  between operations: 16.6 us -> 1.29 us
    all_to_all x1 -> x0, blocking collectives: 341 us -> none  [local_step(): received = lax.all_to_all(grad_parts, 'dp', 0, 0, tiled=True)]
    all_to_all x1 -> x0, other arithmetic: 299 us -> none  [local_step(): received = lax.all_to_all(grad_parts, 'dp', 0, 0, tiled=True)]
    all_gather x1 -> x0, other arithmetic: 299 us -> none  [local_step(): params = lax.all_gather(new_master.astype(jnp.bfloat16), 'dp', tiled=True)]
    pallas_call x0 -> x2, Pallas kernels: none -> 207 us  [the longest x1 200 us: local_step(): pl.pallas_call(functools.partial(kernel, rows), out_shape=(pltpu.VMEM(who...]
    all_gather x1 -> x0, waiting for transfers between devices: 177 us -> none  [local_step(): params = lax.all_gather(new_master.astype(jnp.bfloat16), 'dp', tiled=True)]
    unnamed x8 -> x0, local copies, waits for them, and re-layouts: 81.5 us -> none
    psum x1 -> x0, blocking collectives: 39.5 us -> none  [local_step(): sq_total = lax.psum(jnp.sum(grad_mean * grad_mean), 'dp')]
    reduce_sum x2 -> x0, other arithmetic: 34.3 us -> none  [the longest x1 33.4 us: local_step(): grad_mean = jnp.sum(received, axis=0, dtype=jnp.float32) / num_dev]
  transfers between devices with their start and end apart: 1 -> 0, of which waited for: 1 -> 0; matrix products, arithmetic and copies ran while one was open for 0% -> 0% of each run, Pallas kernels for 0% -> 0%
where the time goes in v3:
time: 208 us
  Pallas kernels  207 us (100%)
    pallas_call x1, Pallas kernels, local_step(): pl.pallas_call(functools.partial(kernel, rows), out_shape=(pltpu.VMEM(who...  200 us
    pallas_call x1, Pallas kernels, local_step(): pl.pallas_call(write_out, out_shape=(jax.ShapeDtypeStruct(whole, BF16), s...  6.49 us

profile of v3, /device:TPU:0, one launch (start us, length us, event | category | flops | bytes accessed | tf_op | source)
XLA Modules:
  0.0 207.9 jit_solution(17117328225572268963)
XLA Ops:
  1.3 200.1 %shard_map.101 = (bf16[29376,2,128]{2,1,0:T(2,128)(2,1)S(1)}, f32[1836,128]{1,0:T(8,128)S(1)}, f32[1836,128]{1,0:T(8,128)S(1)}, f32[1836,128]{1,0:T(8,128)S(1)}, f32[1,128]{1,0:T(1,128)S(1)}) custom-call(bf16[1,7520256]{1,0:T(2,128)(2,1)} %grad_hbm.1, f32[1836,128]{1,0:T(8,128)} %bitcast.10, f32[1836,128]{1,0:T(8,128)} %bitcast.11, f32[1836,128]{1,0:T(8,128)} %bitcast.12, ...), custom_call_target="tpu_custom_call" | custom-call | tf_op jit(solution)/shard_map/pallas_call | solution.py:422
  201.4 6.5 %shard_map.102 = (bf16[29376,2,128]{2,1,0:T(2,128)(2,1)}, f32[1836,128]{1,0:T(8,128)}, f32[1836,128]{1,0:T(8,128)}, f32[1836,128]{1,0:T(8,128)}, f32[1,128]{1,0:T(1,128)}) custom-call(bf16[29376,2,128]{2,1,0:T(2,128)(2,1)S(1)} %get-tuple-element.15.refs_0_, f32[1836,128]{1,0:T(8,128)S(1)} %get-tuple-element.16.refs_1_, ...), custom_call_target="tpu_custom_call" | custom-call | tf_op jit(solution)/shard_map/pallas_call | solution.py:444

commit v4 on v3

--- a/solution.py
+++ b/solution.py
@@ -30,52 +30,59 @@
 REDUCE_TILES = (47, 47, 20)
 SPAN_OF = (0, 0, 1)
 GATHER = (
-    ((X, Y, LOW, HIGH), ((0, 1), (1, 0), (1, 1), (0, 0))),
-    ((Y, X, LOW, HIGH), ((0, 1), (1, 0), (1, 1), (0, 0))),
-    ((LOW, HIGH, X, Y), ((0, 1), (1, 0), (1, 1), (0, 0))),
+    ((X, Y, LOW, HIGH), ((1, 1), (0, 1), (1, 0), (0, 0))),
+    ((Y, X, LOW, HIGH), ((1, 1), (0, 1), (1, 0), (0, 0))),
+    ((LOW, HIGH, X, Y), ((1, 0), (1, 1), (0, 1), (0, 0))),
 )
 GATHER_TILES = (48, 48, 18)
 REDUCE_ORDER = (
-    (0, 1, 0, 1, 1, 1), (1, 2, 0, 1, 2, -1), (0, 0, 0, 1, 1, 1), (1, 0, 0, 1, 2, -1), (1, 1, 0, 1, 2, -1),
-    (0, 1, 0, 1, 1, 0), (1, 2, 0, 1, 1, -1), (0, 0, 0, 1, 1, 0), (1, 0, 0, 1, 1, -1), (1, 1, 0, 1, 1, -1),
-    (0, 1, 0, 1, 0, 1), (1, 2, 0, 1, 0, -1), (0, 0, 0, 1, 0, 1), (1, 0, 0, 1, 0, -1), (1, 1, 0, 0, 2, -1),
-    (0, 1, 0, 1, 0, 0), (0, 0, 0, 1, 0, 0), (1, 1, 0, 0, 1, -1), (0, 1, 0, 0, 1, 1), (1, 2, 0, 0, 2, -1),
-    (0, 0, 0, 0, 1, 1), (1, 1, 0, 1, 0, -1), (1, 0, 0, 0, 2, -1), (0, 1, 0, 0, 1, 0), (1, 2, 0, 0, 1, -1),
-    (0, 0, 0, 0, 1, 0), (1, 0, 0, 0, 1, -1), (0, 1, 0, 0, 0, 1), (1, 2, 0, 0, 0, -1), (0, 0, 0, 0, 0, 1),
-    (1, 0, 0, 0, 0, -1), (1, 1, 0, 0, 0, -1), (0, 1, 0, 0, 0, 0), (0, 0, 0, 0, 0, 0), (0, 1, 1, 1, 1, 1),
-    (1, 2, 1, 1, 2, -1), (0, 0, 1, 1, 1, 1), (0, 1, 1, 1, 1, 0), (1, 2, 1, 1, 1, -1), (0, 0, 1, 1, 1, 0),
-    (0, 1, 1, 1, 0, 1), (1, 2, 1, 1, 0, -1), (0, 0, 1, 1, 0, 1), (0, 1, 1, 1, 0, 0), (0, 0, 1, 1, 0, 0), (2, 2, 0),
-    (0, 1, 1, 0, 1, 1), (1, 2, 1, 0, 2, 0), (0, 0, 1, 0, 1, 1), (0, 1, 1, 0, 1, 0), (1, 2, 1, 0, 1, 0),
-    (0, 0, 1, 0, 1, 0), (0, 1, 1, 0, 0, 1), (1, 2, 1, 0, 0, 0), (0, 0, 1, 0, 0, 1), (0, 1, 1, 0, 0, 0),
-    (0, 0, 1, 0, 0, 0), (0, 1, 2, 1, 1, 1), (0, 0, 2, 1, 1, 1), (0, 1, 2, 1, 1, 0), (0, 0, 2, 1, 1, 0),
-    (0, 1, 2, 1, 0, 1), (0, 0, 2, 1, 0, 1), (0, 1, 2, 1, 0, 0), (0, 0, 2, 1, 0, 0), (0, 1, 2, 0, 1, 1),
-    (0, 0, 2, 0, 1, 1), (0, 1, 2, 0, 1, 0), (0, 0, 2, 0, 1, 0), (2, 0, 0), (2, 1, 0), (3, 2, 0), (1, 0, 1, 1, 2, 0),
-    (1, 1, 1, 1, 2, 0), (0, 1, 2, 0, 0, 1), (1, 0, 1, 1, 1, 0), (1, 1, 1, 1, 1, 0), (1, 0, 1, 1, 0, 0),
-    (1, 1, 1, 1, 0, 0), (1, 2, 2, 1, 2, 1), (1, 2, 2, 1, 1, 1), (1, 2, 2, 1, 0, 1), (0, 0, 2, 0, 0, 1),
-    (0, 1, 2, 0, 0, 0), (0, 0, 2, 0, 0, 0), (0, 1, 3, 1, 1, 1), (0, 0, 3, 1, 1, 1), (0, 1, 3, 1, 1, 0),
-    (0, 0, 3, 1, 1, 0), (0, 1, 3, 1, 0, 1), (0, 0, 3, 1, 0, 1), (0, 1, 3, 1, 0, 0), (0, 0, 3, 1, 0, 0),
-    (0, 1, 3, 0, 1, 1), (0, 0, 3, 0, 1, 1), (0, 1, 3, 0, 1, 0), (0, 0, 3, 0, 1, 0), (0, 1, 3, 0, 0, 1),
-    (0, 0, 3, 0, 0, 1), (0, 1, 3, 0, 0, 0), (0, 0, 3, 0, 0, 0), (2, 2, 1), (1, 2, 2, 0, 2, 2), (1, 2, 2, 0, 1, 2),
-    (1, 2, 2, 0, 0, 2), (3, 0, 0), (3, 1, 0), (1, 0, 1, 0, 2, 1), (1, 1, 1, 0, 2, 1), (1, 0, 1, 0, 1, 1),
-    (1, 1, 1, 0, 1, 1), (1, 0, 1, 0, 0, 1), (1, 1, 1, 0, 0, 1), (4, 2, 0), (3, 2, 1), (1, 2, 3, 1, 2, 3),
-    (1, 2, 3, 1, 1, 3), (1, 2, 3, 1, 0, 3), (4, 1, 0), (4, 0, 0), (2, 2, 2), (1, 2, 3, 0, 2, 4), (1, 2, 3, 0, 1, 4),
-    (1, 2, 3, 0, 0, 4), (4, 2, 1), (2, 0, 1), (2, 1, 1), (1, 0, 2, 1, 2, 2), (1, 1, 2, 1, 2, 2), (1, 0, 2, 1, 1, 2),
-    (1, 1, 2, 1, 1, 2), (1, 0, 2, 1, 0, 2), (1, 1, 2, 1, 0, 2), (3, 2, 2), (2, 2, 3), (3, 0, 1), (1, 0, 2, 0, 2, 3),
-    (1, 0, 2, 0, 1, 3), (1, 0, 2, 0, 0, 3), (3, 1, 1), (1, 1, 2, 0, 2, 3), (1, 1, 2, 0, 1, 3), (1, 1, 2, 0, 0, 3),
-    (4, 1, 1), (4, 0, 1), (2, 0, 2), (2, 1, 2), (1, 0, 3, 1, 2, 4), (1, 1, 3, 1, 2, 4), (1, 0, 3, 1, 1, 4),
-    (1, 1, 3, 1, 1, 4), (1, 0, 3, 1, 0, 4), (1, 1, 3, 1, 0, 4), (3, 0, 2), (3, 1, 2), (1, 0, 3, 0, 2, 5),
-    (1, 1, 3, 0, 2, 5), (1, 0, 3, 0, 1, 5), (1, 1, 3, 0, 1, 5), (1, 0, 3, 0, 0, 5), (1, 1, 3, 0, 0, 5), (4, 2, 2),
-    (4, 1, 2), (3, 2, 3), (4, 0, 2), (4, 2, 3), (2, 0, 3), (2, 1, 3), (3, 0, 3), (5, 2, 0), (3, 1, 3), (4, 1, 3),
-    (4, 0, 3), (5, 1, 0), (5, 0, 0),
+    (0, 1, 0, 1, 1, 1), (0, 0, 0, 1, 1, 1), (1, 0, 0, 1, 2), (1, 1, 0, 1, 2), (0, 1, 0, 1, 1, 0), (1, 2, 0, 1, 2),
+    (0, 0, 0, 1, 1, 0), (1, 0, 0, 1, 1), (0, 1, 0, 1, 0, 1), (0, 0, 0, 1, 0, 1), (0, 1, 0, 1, 0, 0),
+    (0, 0, 0, 1, 0, 0), (1, 1, 0, 0, 1), (1, 2, 0, 1, 1), (0, 1, 0, 0, 1, 1), (0, 0, 0, 0, 1, 1),
+    (0, 1, 0, 0, 1, 0), (0, 0, 0, 0, 1, 0), (1, 2, 0, 0, 1), (0, 1, 0, 0, 0, 1), (0, 0, 0, 0, 0, 1),
+    (0, 1, 0, 0, 0, 0), (0, 0, 0, 0, 0, 0), (0, 1, 1, 1, 1, 1), (0, 0, 1, 1, 1, 1), (1, 1, 0, 1, 1),
+    (1, 1, 0, 1, 0), (1, 0, 0, 0, 2), (0, 1, 1, 1, 1, 0), (1, 2, 1, 1, 1), (0, 0, 1, 1, 1, 0), (1, 2, 0, 0, 2),
+    (1, 0, 0, 1, 0), (1, 2, 0, 0, 0), (0, 1, 1, 1, 0, 1), (1, 0, 0, 0, 1), (1, 2, 1, 1, 0), (1, 2, 0, 1, 0),
+    (1, 1, 0, 0, 2), (0, 0, 1, 1, 0, 1), (0, 1, 1, 1, 0, 0), (1, 1, 0, 0, 0), (0, 0, 1, 1, 0, 0), (1, 1, 1, 1, 1),
+    (0, 1, 1, 0, 1, 1), (0, 0, 1, 0, 1, 1), (0, 1, 1, 0, 1, 0), (0, 0, 1, 0, 1, 0), (0, 1, 1, 0, 0, 1),
+    (0, 0, 1, 0, 0, 1), (0, 1, 1, 0, 0, 0), (2, 2, 0), (0, 0, 1, 0, 0, 0), (1, 2, 1, 0, 2), (0, 1, 2, 1, 1, 1),
+    (0, 0, 2, 1, 1, 1), (1, 2, 1, 1, 2), (1, 1, 2, 1, 2), (1, 0, 1, 1, 0), (0, 1, 2, 1, 1, 0), (3, 2, 0),
+    (1, 2, 1, 0, 0), (0, 0, 2, 1, 1, 0), (0, 1, 2, 1, 0, 1), (0, 0, 2, 1, 0, 1), (4, 2, 0), (2, 1, 0), (3, 1, 0),
+    (0, 1, 2, 1, 0, 0), (0, 0, 2, 1, 0, 0), (2, 0, 0), (1, 1, 1, 0, 1), (0, 1, 2, 0, 1, 1), (1, 0, 1, 1, 2),
+    (1, 2, 2, 1, 2), (0, 0, 2, 0, 1, 1), (1, 2, 2, 1, 0), (0, 1, 2, 0, 1, 0), (0, 0, 2, 0, 1, 0),
+    (0, 1, 2, 0, 0, 1), (1, 0, 2, 0, 1), (3, 0, 0), (0, 0, 2, 0, 0, 1), (1, 2, 2, 1, 1), (1, 0, 0, 0, 0),
+    (1, 1, 2, 0, 0), (1, 0, 2, 1, 0), (1, 2, 1, 0, 1), (0, 1, 2, 0, 0, 0), (0, 0, 2, 0, 0, 0), (0, 1, 3, 1, 1, 1),
+    (1, 0, 1, 1, 1), (0, 0, 3, 1, 1, 1), (0, 1, 3, 1, 1, 0), (2, 2, 1), (3, 2, 1), (4, 0, 0), (1, 0, 2, 0, 2),
+    (1, 0, 1, 0, 2), (5, 2, 0), (1, 1, 1, 1, 2), (0, 0, 3, 1, 1, 0), (0, 1, 3, 1, 0, 1), (0, 0, 3, 1, 0, 1),
+    (1, 1, 3, 0, 2), (2, 2, 2), (1, 2, 2, 0, 1), (0, 1, 3, 1, 0, 0), (0, 0, 3, 1, 0, 0), (4, 1, 0), (5, 1, 0),
+    (1, 2, 2, 0, 2), (0, 1, 3, 0, 1, 1), (0, 0, 3, 0, 1, 1), (1, 1, 1, 0, 0), (0, 1, 3, 0, 1, 0), (1, 2, 3, 0, 1),
+    (1, 2, 3, 1, 1), (6, 1, 0), (0, 0, 3, 0, 1, 0), (0, 1, 3, 0, 0, 1), (2, 0, 1), (1, 2, 3, 1, 0), (1, 1, 2, 1, 1),
+    (4, 2, 1), (5, 0, 0), (1, 0, 3, 0, 2), (1, 2, 2, 0, 0), (0, 0, 3, 0, 0, 1), (0, 1, 3, 0, 0, 0), (5, 2, 1),
+    (4, 2, 2), (1, 2, 3, 1, 2), (1, 2, 3, 0, 2), (6, 0, 0), (1, 0, 1, 0, 1), (1, 1, 1, 1, 0), (3, 2, 2),
+    (1, 1, 2, 1, 0), (1, 2, 3, 0, 0), (1, 1, 2, 0, 1), (1, 0, 2, 1, 2), (0, 0, 3, 0, 0, 0), (1, 0, 2, 0, 0),
+    (1, 1, 1, 0, 2), (1, 0, 1, 0, 0), (1, 1, 3, 1, 0), (1, 1, 3, 1, 1), (2, 1, 2), (2, 1, 1), (3, 1, 1),
+    (1, 0, 3, 1, 0), (4, 1, 1), (1, 0, 2, 1, 1), (3, 0, 1), (5, 1, 1), (1, 0, 3, 0, 0), (6, 1, 1), (4, 0, 1),
+    (2, 2, 3), (3, 2, 3), (1, 1, 2, 0, 2), (3, 1, 2), (5, 0, 1), (1, 1, 3, 0, 1), (6, 2, 1), (2, 0, 2), (3, 0, 2),
+    (4, 1, 2), (4, 0, 2), (1, 0, 3, 1, 1), (5, 2, 2), (5, 1, 2), (6, 1, 2), (6, 0, 1), (6, 2, 0), (1, 1, 3, 0, 0),
+    (1, 0, 3, 0, 1), (5, 0, 2), (4, 2, 3), (6, 0, 2), (6, 2, 2), (1, 1, 3, 1, 2), (1, 0, 3, 1, 2), (2, 1, 3),
+    (2, 0, 3), (3, 0, 3), (3, 1, 3), (4, 1, 3), (4, 0, 3), (5, 0, 3), (5, 2, 3), (7, 2, 0), (5, 1, 3), (7, 1, 0),
+    (7, 0, 0),
 )
 GATHER_ORDER = (
-    (0, 0, 0, 0), (0, 1, 0, 0), (0, 2, 0, 0), (1, 0, 0, 0), (1, 1, 0, 0), (1, 2, 0, 0), (2, 0, 0, 0), (2, 1, 0, 0),
-    (2, 2, 0, 0), (5, 0, 3, 0), (4, 0, 3, 0), (4, 1, 3, 0), (5, 1, 3, 0), (3, 0, 2, 0), (3, 2, 1, 0), (3, 2, 2, 0),
-    (3, 0, 1, 0), (3, 2, 0, 0), (5, 0, 3, 1), (3, 0, 0, 0), (5, 1, 3, 1), (5, 0, 1, 0), (5, 0, 2, 0), (4, 0, 1, 0),
-    (4, 0, 2, 0), (3, 1, 2, 0), (5, 0, 0, 0), (3, 1, 1, 0), (4, 0, 0, 0), (5, 1, 1, 0), (5, 0, 1, 1), (5, 0, 2, 1),
-    (5, 1, 2, 0), (3, 1, 0, 0), (4, 2, 3, 0), (4, 1, 2, 0), (5, 2, 3, 0), (4, 2, 1, 0), (5, 1, 0, 0), (5, 2, 1, 0),
-    (4, 1, 1, 0), (5, 1, 2, 1), (4, 2, 2, 0), (5, 2, 2, 0), (4, 1, 0, 0), (5, 0, 0, 1), (4, 2, 0, 0), (5, 1, 1, 1),
-    (5, 2, 0, 0), (5, 2, 3, 1), (5, 2, 1, 1), (5, 1, 0, 1), (5, 2, 2, 1), (5, 2, 0, 1),
+    (0, 2, 0), (1, 2, 1), (0, 0, 0), (1, 0, 2), (3, 0, 3, 0), (4, 2, 3, 0, 0), (1, 0, 0), (0, 1, 0), (2, 1, 3),
+    (2, 0, 3), (3, 1, 3, 0), (3, 0, 3, 1), (1, 1, 1), (1, 2, 2), (3, 1, 3, 1), (1, 1, 2), (3, 0, 2, 0),
+    (3, 0, 0, 0), (4, 0, 3, 0, 1), (1, 0, 1), (2, 0, 0), (2, 2, 2), (3, 1, 1, 0), (2, 1, 1), (2, 0, 2),
+    (3, 1, 2, 0), (3, 2, 3, 0), (2, 1, 2), (4, 0, 1, 0, 0), (3, 2, 1, 0), (4, 1, 3, 0, 1), (1, 1, 0), (3, 0, 1, 0),
+    (1, 2, 0), (4, 0, 0, 0, 1), (2, 0, 1), (4, 0, 0, 0, 0), (4, 2, 3, 0, 1), (3, 2, 2, 1), (4, 0, 3, 1, 0),
+    (4, 1, 1, 1, 0), (3, 1, 1, 1), (3, 0, 0, 1), (4, 0, 3, 0, 0), (4, 0, 2, 0, 1), (4, 2, 1, 0, 1), (4, 1, 3, 0, 0),
+    (4, 0, 1, 1, 0), (4, 2, 0, 0, 0), (4, 2, 2, 0, 0), (2, 2, 1), (4, 0, 2, 0, 0), (3, 2, 2, 0), (4, 2, 1, 0, 0),
+    (2, 2, 3), (3, 0, 1, 1), (2, 1, 0), (3, 1, 2, 1), (3, 2, 1, 1), (4, 1, 1, 0, 1), (4, 2, 2, 1, 1), (3, 0, 2, 1),
+    (4, 0, 1, 0, 1), (4, 1, 1, 1, 1), (2, 2, 0), (4, 1, 2, 1, 0), (3, 2, 0, 0), (4, 0, 0, 1, 0), (3, 1, 0, 0),
+    (4, 0, 2, 1, 0), (4, 1, 3, 1, 1), (4, 1, 2, 1, 1), (4, 1, 3, 1, 0), (4, 2, 1, 1, 1), (4, 0, 1, 1, 1),
+    (3, 1, 0, 1), (4, 0, 0, 1, 1), (4, 2, 2, 0, 1), (4, 2, 1, 1, 0), (4, 1, 2, 0, 1), (4, 1, 0, 0, 1),
+    (4, 1, 2, 0, 0), (3, 2, 3, 1), (3, 2, 0, 1), (4, 2, 2, 1, 0), (4, 1, 0, 1, 0), (4, 2, 3, 1, 0), (4, 1, 0, 0, 0),
+    (4, 0, 2, 1, 1), (4, 0, 3, 1, 1), (4, 1, 1, 0, 0), (4, 2, 0, 1, 0), (4, 2, 3, 1, 1), (4, 1, 0, 1, 1),
+    (4, 2, 0, 0, 1), (4, 2, 0, 1, 1),
 )
 HALF = ((1, 1), (1, 0), (0, 1), (0, 0))
 
@@ -225,7 +232,6 @@
 
         if g < 3:
             over_rows(part[c], 4, body)
-            third_copy(c, g).start()
 
     def final(c, acc):
         for g in range(3):
@@ -277,18 +283,17 @@
             if not entered:
                 pl.semaphore_wait(barrier, 31)
                 entered = True
-            j2, slot, h = task[3:]
-            if h >= 0:
-                for other in range(3):
-                    need(first_copy, c, h // 2, 1 - h % 2, other)
-            first_copy(c, g, j2, slot).start()
+            first_copy(c, g, *task[3:]).start()
         elif kind == 2:
             four_sum(c, g, 1, sent2[c])
+        elif kind == 3:
             second_copy(c, g).start()
-        elif kind == 3:
+        elif kind == 4:
             four_sum(c, g, 0, kept[c])
-        elif kind == 4:
+        elif kind == 5:
             plane_sum(c, g)
+        elif kind == 6:
+            third_copy(c, g).start()
         else:
             acc = final(c, acc)
 
@@ -350,28 +355,19 @@
         spot = piece(c, g, j2, j1)
         return send(spot, spot, gs4.at[c, g, j2, j1], gr4.at[c, g, j2, j1], (CORE,))
 
-    for kind, c, g, j2 in GATHER_ORDER:
+    for kind, c, *key in GATHER_ORDER:
         if kind == 0:
             update(c)
         elif kind == 1:
-            for group in (2, 1, 0):
-                gather1(c, group).start()
-            gather2(c, 3).start()
-            gather3(c, 3, 0).start()
-        elif kind == 2:
-            gather4(c, 3, 0, 0).start()
-        elif kind == 3:
-            gather1_in(c, g).wait_recv()
-            gather2(c, g).start()
-            gather3(c, g, 0).start()
-            gather4(c, g, 0, 0).start()
-        elif kind == 4:
-            gather2(c, g).wait_recv()
-            gather3(c, g, 1).start()
-            gather4(c, g, 1, 0).start()
+            gather1(c, *key).start()
         else:
-            gather3(c, g, j2).wait_recv()
-            gather4(c, g, j2, 1).start()
+            if kind == 4 and key[2]:
+                need(gather3, c, *key[:2])
+            elif kind > 2 and key[1]:
+                need(gather2, c, key[0])
+            elif key[0] < 3:
+                need(gather1_in, c, key[0])
+            (gather2, gather3, gather4)[kind - 2](c, *key).start()
 
     for c in range(count):
         for g in range(4):

time: 208 us -> 199 us (0.957)
  Pallas kernels: 207 us -> 197 us
    pallas_call x1, Pallas kernels: 200 us -> 191 us  [local_step(): pl.pallas_call(functools.partial(kernel, rows), out_shape=(pltpu.VMEM(who...]
where the time goes in v4:
time: 199 us
  Pallas kernels  197 us (99%)
    pallas_call x1, Pallas kernels, local_step(): pl.pallas_call(functools.partial(kernel, rows), out_shape=(pltpu.VMEM(who...  191 us
    pallas_call x1, Pallas kernels, local_step(): pl.pallas_call(write_out, out_shape=(jax.ShapeDtypeStruct(whole, BF16), s...  6.49 us

profile of v4, /device:TPU:0, one launch (start us, length us, event | category | flops | bytes accessed | tf_op | source)
XLA Modules:
  0.0 198.6 jit_solution(13758892090755841430)
XLA Ops:
  1.3 190.9 %shard_map.101 = (bf16[29376,2,128]{2,1,0:T(2,128)(2,1)S(1)}, f32[1836,128]{1,0:T(8,128)S(1)}, f32[1836,128]{1,0:T(8,128)S(1)}, f32[1836,128]{1,0:T(8,128)S(1)}, f32[1,128]{1,0:T(1,128)S(1)}) custom-call(bf16[1,7520256]{1,0:T(2,128)(2,1)} %grad_hbm.1, f32[1836,128]{1,0:T(8,128)} %bitcast.10, f32[1836,128]{1,0:T(8,128)} %bitcast.11, f32[1836,128]{1,0:T(8,128)} %bitcast.12, ...), custom_call_target="tpu_custom_call" | custom-call | tf_op jit(solution)/shard_map/pallas_call | solution.py:418
  192.1 6.5 %shard_map.102 = (bf16[29376,2,128]{2,1,0:T(2,128)(2,1)}, f32[1836,128]{1,0:T(8,128)}, f32[1836,128]{1,0:T(8,128)}, f32[1836,128]{1,0:T(8,128)}, f32[1,128]{1,0:T(1,128)}) custom-call(bf16[29376,2,128]{2,1,0:T(2,128)(2,1)S(1)} %get-tuple-element.15.refs_0_, f32[1836,128]{1,0:T(8,128)S(1)} %get-tuple-element.16.refs_1_, ...), custom_call_target="tpu_custom_call" | custom-call | tf_op jit(solution)/shard_map/pallas_call | solution.py:440

commit v5 on v4

--- a/solution.py
+++ b/solution.py
@@ -16,6 +16,7 @@
 LANES = 128
 TILE = 16
 STAGES = 4
+CHUNKS = 8
 VMEM_LIMIT = 46 * 1024 * 1024
 MESH = pl.DeviceIdType.MESH
 F32 = jnp.float32
@@ -36,52 +37,52 @@
 )
 GATHER_TILES = (48, 48, 18)
 REDUCE_ORDER = (
-    (0, 1, 0, 1, 1, 1), (0, 0, 0, 1, 1, 1), (1, 0, 0, 1, 2), (1, 1, 0, 1, 2), (0, 1, 0, 1, 1, 0), (1, 2, 0, 1, 2),
-    (0, 0, 0, 1, 1, 0), (1, 0, 0, 1, 1), (0, 1, 0, 1, 0, 1), (0, 0, 0, 1, 0, 1), (0, 1, 0, 1, 0, 0),
-    (0, 0, 0, 1, 0, 0), (1, 1, 0, 0, 1), (1, 2, 0, 1, 1), (0, 1, 0, 0, 1, 1), (0, 0, 0, 0, 1, 1),
-    (0, 1, 0, 0, 1, 0), (0, 0, 0, 0, 1, 0), (1, 2, 0, 0, 1), (0, 1, 0, 0, 0, 1), (0, 0, 0, 0, 0, 1),
-    (0, 1, 0, 0, 0, 0), (0, 0, 0, 0, 0, 0), (0, 1, 1, 1, 1, 1), (0, 0, 1, 1, 1, 1), (1, 1, 0, 1, 1),
-    (1, 1, 0, 1, 0), (1, 0, 0, 0, 2), (0, 1, 1, 1, 1, 0), (1, 2, 1, 1, 1), (0, 0, 1, 1, 1, 0), (1, 2, 0, 0, 2),
-    (1, 0, 0, 1, 0), (1, 2, 0, 0, 0), (0, 1, 1, 1, 0, 1), (1, 0, 0, 0, 1), (1, 2, 1, 1, 0), (1, 2, 0, 1, 0),
-    (1, 1, 0, 0, 2), (0, 0, 1, 1, 0, 1), (0, 1, 1, 1, 0, 0), (1, 1, 0, 0, 0), (0, 0, 1, 1, 0, 0), (1, 1, 1, 1, 1),
-    (0, 1, 1, 0, 1, 1), (0, 0, 1, 0, 1, 1), (0, 1, 1, 0, 1, 0), (0, 0, 1, 0, 1, 0), (0, 1, 1, 0, 0, 1),
-    (0, 0, 1, 0, 0, 1), (0, 1, 1, 0, 0, 0), (2, 2, 0), (0, 0, 1, 0, 0, 0), (1, 2, 1, 0, 2), (0, 1, 2, 1, 1, 1),
-    (0, 0, 2, 1, 1, 1), (1, 2, 1, 1, 2), (1, 1, 2, 1, 2), (1, 0, 1, 1, 0), (0, 1, 2, 1, 1, 0), (3, 2, 0),
-    (1, 2, 1, 0, 0), (0, 0, 2, 1, 1, 0), (0, 1, 2, 1, 0, 1), (0, 0, 2, 1, 0, 1), (4, 2, 0), (2, 1, 0), (3, 1, 0),
-    (0, 1, 2, 1, 0, 0), (0, 0, 2, 1, 0, 0), (2, 0, 0), (1, 1, 1, 0, 1), (0, 1, 2, 0, 1, 1), (1, 0, 1, 1, 2),
-    (1, 2, 2, 1, 2), (0, 0, 2, 0, 1, 1), (1, 2, 2, 1, 0), (0, 1, 2, 0, 1, 0), (0, 0, 2, 0, 1, 0),
-    (0, 1, 2, 0, 0, 1), (1, 0, 2, 0, 1), (3, 0, 0), (0, 0, 2, 0, 0, 1), (1, 2, 2, 1, 1), (1, 0, 0, 0, 0),
-    (1, 1, 2, 0, 0), (1, 0, 2, 1, 0), (1, 2, 1, 0, 1), (0, 1, 2, 0, 0, 0), (0, 0, 2, 0, 0, 0), (0, 1, 3, 1, 1, 1),
-    (1, 0, 1, 1, 1), (0, 0, 3, 1, 1, 1), (0, 1, 3, 1, 1, 0), (2, 2, 1), (3, 2, 1), (4, 0, 0), (1, 0, 2, 0, 2),
-    (1, 0, 1, 0, 2), (5, 2, 0), (1, 1, 1, 1, 2), (0, 0, 3, 1, 1, 0), (0, 1, 3, 1, 0, 1), (0, 0, 3, 1, 0, 1),
-    (1, 1, 3, 0, 2), (2, 2, 2), (1, 2, 2, 0, 1), (0, 1, 3, 1, 0, 0), (0, 0, 3, 1, 0, 0), (4, 1, 0), (5, 1, 0),
-    (1, 2, 2, 0, 2), (0, 1, 3, 0, 1, 1), (0, 0, 3, 0, 1, 1), (1, 1, 1, 0, 0), (0, 1, 3, 0, 1, 0), (1, 2, 3, 0, 1),
-    (1, 2, 3, 1, 1), (6, 1, 0), (0, 0, 3, 0, 1, 0), (0, 1, 3, 0, 0, 1), (2, 0, 1), (1, 2, 3, 1, 0), (1, 1, 2, 1, 1),
-    (4, 2, 1), (5, 0, 0), (1, 0, 3, 0, 2), (1, 2, 2, 0, 0), (0, 0, 3, 0, 0, 1), (0, 1, 3, 0, 0, 0), (5, 2, 1),
-    (4, 2, 2), (1, 2, 3, 1, 2), (1, 2, 3, 0, 2), (6, 0, 0), (1, 0, 1, 0, 1), (1, 1, 1, 1, 0), (3, 2, 2),
-    (1, 1, 2, 1, 0), (1, 2, 3, 0, 0), (1, 1, 2, 0, 1), (1, 0, 2, 1, 2), (0, 0, 3, 0, 0, 0), (1, 0, 2, 0, 0),
-    (1, 1, 1, 0, 2), (1, 0, 1, 0, 0), (1, 1, 3, 1, 0), (1, 1, 3, 1, 1), (2, 1, 2), (2, 1, 1), (3, 1, 1),
-    (1, 0, 3, 1, 0), (4, 1, 1), (1, 0, 2, 1, 1), (3, 0, 1), (5, 1, 1), (1, 0, 3, 0, 0), (6, 1, 1), (4, 0, 1),
-    (2, 2, 3), (3, 2, 3), (1, 1, 2, 0, 2), (3, 1, 2), (5, 0, 1), (1, 1, 3, 0, 1), (6, 2, 1), (2, 0, 2), (3, 0, 2),
-    (4, 1, 2), (4, 0, 2), (1, 0, 3, 1, 1), (5, 2, 2), (5, 1, 2), (6, 1, 2), (6, 0, 1), (6, 2, 0), (1, 1, 3, 0, 0),
-    (1, 0, 3, 0, 1), (5, 0, 2), (4, 2, 3), (6, 0, 2), (6, 2, 2), (1, 1, 3, 1, 2), (1, 0, 3, 1, 2), (2, 1, 3),
-    (2, 0, 3), (3, 0, 3), (3, 1, 3), (4, 1, 3), (4, 0, 3), (5, 0, 3), (5, 2, 3), (7, 2, 0), (5, 1, 3), (7, 1, 0),
-    (7, 0, 0),
+    (0, 1, 0, 1, 1, 1), (0, 0, 0, 1, 1, 1), (1, 1, 0, 1, 2), (1, 0, 0, 1, 2), (0, 1, 0, 1, 1, 0), (1, 2, 0, 1, 1),
+    (0, 0, 0, 1, 1, 0), (0, 1, 0, 1, 0, 1), (1, 2, 0, 1, 2), (1, 1, 0, 1, 1), (1, 2, 0, 1, 0), (0, 0, 0, 1, 0, 1),
+    (0, 1, 0, 1, 0, 0), (0, 0, 0, 1, 0, 0), (0, 1, 0, 0, 1, 1), (0, 0, 0, 0, 1, 1), (0, 1, 0, 0, 1, 0),
+    (0, 0, 0, 0, 1, 0), (1, 0, 0, 0, 1), (0, 1, 0, 0, 0, 1), (0, 0, 0, 0, 0, 1), (0, 1, 0, 0, 0, 0),
+    (0, 0, 0, 0, 0, 0), (0, 1, 1, 1, 1, 1), (0, 0, 1, 1, 1, 1), (1, 2, 1, 1, 2), (0, 1, 1, 1, 1, 0),
+    (1, 2, 1, 1, 1), (0, 0, 1, 1, 1, 0), (0, 1, 1, 1, 0, 1), (0, 0, 1, 1, 0, 1), (0, 1, 1, 1, 0, 0),
+    (1, 0, 0, 1, 0), (0, 0, 1, 1, 0, 0), (0, 1, 1, 0, 1, 1), (2, 2, 0), (0, 0, 1, 0, 1, 1), (0, 1, 1, 0, 1, 0),
+    (1, 2, 0, 0, 2), (1, 1, 0, 0, 2), (0, 0, 1, 0, 1, 0), (0, 1, 1, 0, 0, 1), (0, 0, 1, 0, 0, 1), (1, 1, 0, 1, 0),
+    (1, 0, 0, 1, 1), (0, 1, 1, 0, 0, 0), (1, 1, 1, 1, 0), (0, 0, 1, 0, 0, 0), (0, 1, 2, 1, 1, 1),
+    (0, 0, 2, 1, 1, 1), (2, 1, 0), (3, 2, 0), (1, 2, 1, 1, 0), (1, 0, 0, 0, 2), (3, 1, 0), (0, 1, 2, 1, 1, 0),
+    (0, 0, 2, 1, 1, 0), (0, 1, 2, 1, 0, 1), (1, 2, 2, 1, 1), (1, 1, 0, 0, 1), (1, 2, 2, 1, 2), (0, 0, 2, 1, 0, 1),
+    (0, 1, 2, 1, 0, 0), (0, 0, 2, 1, 0, 0), (1, 1, 2, 0, 1), (1, 1, 1, 0, 0), (0, 1, 2, 0, 1, 1),
+    (0, 0, 2, 0, 1, 1), (0, 1, 2, 0, 1, 0), (2, 0, 0), (3, 0, 0), (1, 1, 2, 1, 0), (2, 2, 1), (1, 0, 0, 0, 0),
+    (1, 1, 1, 0, 2), (1, 2, 0, 0, 0), (1, 0, 2, 0, 2), (1, 1, 0, 0, 0), (0, 0, 2, 0, 1, 0), (1, 1, 2, 0, 2),
+    (0, 1, 2, 0, 0, 1), (0, 0, 2, 0, 0, 1), (0, 1, 2, 0, 0, 0), (0, 0, 2, 0, 0, 0), (1, 0, 1, 0, 0),
+    (0, 1, 3, 1, 1, 1), (3, 2, 1), (0, 0, 3, 1, 1, 1), (1, 0, 1, 1, 0), (1, 2, 2, 0, 0), (0, 1, 3, 1, 1, 0),
+    (1, 2, 3, 1, 1), (0, 0, 3, 1, 1, 0), (0, 1, 3, 1, 0, 1), (1, 0, 2, 0, 1), (1, 1, 1, 1, 1), (1, 2, 2, 1, 0),
+    (1, 1, 1, 1, 2), (1, 1, 2, 1, 1), (1, 1, 1, 0, 1), (2, 2, 2), (1, 0, 1, 1, 1), (1, 2, 2, 0, 2),
+    (0, 0, 3, 1, 0, 1), (1, 2, 3, 1, 0), (1, 1, 2, 0, 0), (0, 1, 3, 1, 0, 0), (1, 2, 1, 0, 2), (0, 0, 3, 1, 0, 0),
+    (1, 0, 1, 1, 2), (1, 2, 3, 1, 2), (1, 0, 2, 0, 0), (0, 1, 3, 0, 1, 1), (1, 0, 1, 0, 1), (0, 0, 3, 0, 1, 1),
+    (1, 2, 3, 0, 2), (1, 0, 1, 0, 2), (1, 1, 3, 1, 0), (0, 1, 3, 0, 1, 0), (1, 2, 3, 0, 1), (0, 0, 3, 0, 1, 0),
+    (0, 1, 3, 0, 0, 1), (1, 1, 2, 1, 2), (1, 2, 2, 0, 1), (1, 2, 0, 0, 1), (1, 0, 2, 1, 0), (1, 2, 1, 0, 0),
+    (1, 2, 1, 0, 1), (0, 0, 3, 0, 0, 1), (1, 1, 3, 0, 0), (1, 1, 3, 0, 1), (1, 0, 3, 0, 0), (1, 0, 2, 1, 1),
+    (4, 0, 0), (1, 1, 3, 0, 2), (4, 1, 0), (5, 1, 0), (6, 1, 0), (5, 0, 0), (6, 0, 0), (4, 2, 1), (5, 2, 1),
+    (1, 2, 3, 0, 0), (4, 2, 0), (2, 1, 1), (3, 1, 1), (1, 1, 3, 1, 1), (0, 1, 3, 0, 0, 0), (4, 2, 3),
+    (1, 0, 2, 1, 2), (2, 2, 3), (2, 1, 2), (3, 2, 2), (0, 0, 3, 0, 0, 0), (4, 0, 2), (1, 0, 3, 1, 0), (3, 1, 2),
+    (2, 0, 1), (5, 2, 0), (4, 2, 2), (1, 0, 3, 1, 1), (3, 2, 3), (1, 0, 3, 1, 2), (3, 0, 1), (1, 0, 3, 0, 1),
+    (4, 1, 1), (6, 2, 1), (5, 1, 1), (6, 1, 1), (4, 1, 2), (6, 2, 0), (2, 0, 2), (3, 0, 2), (5, 1, 2), (4, 1, 3),
+    (6, 1, 2), (4, 0, 1), (5, 0, 1), (6, 0, 1), (1, 1, 3, 1, 2), (5, 2, 2), (5, 0, 2), (6, 0, 2), (2, 0, 3),
+    (3, 0, 3), (1, 0, 3, 0, 2), (2, 1, 3), (3, 1, 3), (4, 0, 3), (5, 0, 3), (6, 2, 2), (5, 2, 3), (7, 2, 0),
+    (5, 1, 3), (7, 1, 0), (7, 0, 0),
 )
 GATHER_ORDER = (
-    (0, 2, 0), (1, 2, 1), (0, 0, 0), (1, 0, 2), (3, 0, 3, 0), (4, 2, 3, 0, 0), (1, 0, 0), (0, 1, 0), (2, 1, 3),
+    (0, 2, 0), (1, 2, 1), (0, 0, 0), (3, 0, 3, 0), (1, 0, 2), (4, 2, 3, 0, 0), (1, 0, 0), (0, 1, 0), (2, 1, 3),
     (2, 0, 3), (3, 1, 3, 0), (3, 0, 3, 1), (1, 1, 1), (1, 2, 2), (3, 1, 3, 1), (1, 1, 2), (3, 0, 2, 0),
-    (3, 0, 0, 0), (4, 0, 3, 0, 1), (1, 0, 1), (2, 0, 0), (2, 2, 2), (3, 1, 1, 0), (2, 1, 1), (2, 0, 2),
+    (3, 0, 0, 0), (4, 0, 3, 0, 1), (1, 0, 1), (2, 0, 0), (2, 2, 2), (3, 1, 1, 0), (2, 1, 1), (2, 0, 2), (1, 2, 0),
     (3, 1, 2, 0), (3, 2, 3, 0), (2, 1, 2), (4, 0, 1, 0, 0), (3, 2, 1, 0), (4, 1, 3, 0, 1), (1, 1, 0), (3, 0, 1, 0),
-    (1, 2, 0), (4, 0, 0, 0, 1), (2, 0, 1), (4, 0, 0, 0, 0), (4, 2, 3, 0, 1), (3, 2, 2, 1), (4, 0, 3, 1, 0),
-    (4, 1, 1, 1, 0), (3, 1, 1, 1), (3, 0, 0, 1), (4, 0, 3, 0, 0), (4, 0, 2, 0, 1), (4, 2, 1, 0, 1), (4, 1, 3, 0, 0),
-    (4, 0, 1, 1, 0), (4, 2, 0, 0, 0), (4, 2, 2, 0, 0), (2, 2, 1), (4, 0, 2, 0, 0), (3, 2, 2, 0), (4, 2, 1, 0, 0),
-    (2, 2, 3), (3, 0, 1, 1), (2, 1, 0), (3, 1, 2, 1), (3, 2, 1, 1), (4, 1, 1, 0, 1), (4, 2, 2, 1, 1), (3, 0, 2, 1),
-    (4, 0, 1, 0, 1), (4, 1, 1, 1, 1), (2, 2, 0), (4, 1, 2, 1, 0), (3, 2, 0, 0), (4, 0, 0, 1, 0), (3, 1, 0, 0),
-    (4, 0, 2, 1, 0), (4, 1, 3, 1, 1), (4, 1, 2, 1, 1), (4, 1, 3, 1, 0), (4, 2, 1, 1, 1), (4, 0, 1, 1, 1),
-    (3, 1, 0, 1), (4, 0, 0, 1, 1), (4, 2, 2, 0, 1), (4, 2, 1, 1, 0), (4, 1, 2, 0, 1), (4, 1, 0, 0, 1),
-    (4, 1, 2, 0, 0), (3, 2, 3, 1), (3, 2, 0, 1), (4, 2, 2, 1, 0), (4, 1, 0, 1, 0), (4, 2, 3, 1, 0), (4, 1, 0, 0, 0),
-    (4, 0, 2, 1, 1), (4, 0, 3, 1, 1), (4, 1, 1, 0, 0), (4, 2, 0, 1, 0), (4, 2, 3, 1, 1), (4, 1, 0, 1, 1),
+    (4, 0, 0, 0, 1), (2, 0, 1), (4, 0, 0, 0, 0), (4, 2, 3, 0, 1), (3, 2, 2, 1), (4, 0, 3, 1, 0), (4, 1, 1, 1, 0),
+    (3, 1, 1, 1), (4, 0, 3, 0, 0), (3, 0, 0, 1), (4, 0, 2, 0, 1), (4, 2, 1, 0, 1), (4, 1, 3, 0, 0), (4, 0, 1, 1, 0),
+    (4, 2, 0, 0, 0), (4, 2, 2, 0, 0), (2, 2, 1), (4, 0, 2, 0, 0), (3, 2, 2, 0), (4, 2, 1, 0, 0), (2, 2, 3),
+    (3, 0, 1, 1), (2, 1, 0), (3, 1, 2, 1), (3, 2, 1, 1), (4, 1, 1, 0, 1), (4, 2, 2, 1, 1), (3, 0, 2, 1),
+    (4, 0, 1, 0, 1), (4, 1, 1, 1, 1), (2, 2, 0), (4, 0, 3, 1, 1), (4, 1, 2, 1, 0), (3, 2, 0, 0), (4, 0, 0, 1, 0),
+    (3, 1, 0, 0), (4, 0, 2, 1, 0), (4, 1, 3, 1, 1), (4, 1, 2, 1, 1), (4, 1, 3, 1, 0), (4, 2, 1, 1, 1),
+    (4, 0, 1, 1, 1), (3, 1, 0, 1), (4, 0, 0, 1, 1), (4, 2, 2, 0, 1), (4, 2, 1, 1, 0), (4, 1, 2, 0, 1),
+    (4, 1, 0, 0, 1), (4, 1, 2, 0, 0), (3, 2, 3, 1), (3, 2, 0, 1), (4, 2, 2, 1, 0), (4, 1, 0, 1, 0), (4, 2, 3, 1, 0),
+    (4, 1, 0, 0, 0), (4, 0, 2, 1, 1), (4, 1, 1, 0, 0), (4, 2, 0, 1, 0), (4, 2, 3, 1, 1), (4, 1, 0, 1, 1),
     (4, 2, 0, 0, 1), (4, 2, 0, 1, 1),
 )
 HALF = ((1, 1), (1, 0), (0, 1), (0, 0))
@@ -297,7 +298,7 @@
         else:
             acc = final(c, acc)
 
-    partial[me] = acc
+    partial[me] = jnp.sum(acc, axis=0, keepdims=True)
 
     def norm_copy(j, owner):
         return send(partial.at[owner], partial.at[owner], ns.at[j], nr.at[j], everyone[j])
@@ -393,7 +394,13 @@
 def write_out(*refs):
     sem = refs[-1]
     count = len(refs) // 2
-    copies = [pltpu.make_async_copy(refs[i], refs[count + i], sem.at[i]) for i in range(count)]
+    length = refs[0].shape[0] // CHUNKS
+    copies = []
+    for i in range(CHUNKS):
+        near = pl.ds(i * length, length)
+        copies.append(pltpu.make_async_copy(refs[0].at[near], refs[count].at[near], sem.at[i]))
+    for i in range(1, count):
+        copies.append(pltpu.make_async_copy(refs[i], refs[count + i], sem.at[CHUNKS + i - 1]))
     for copy in copies:
         copy.start()
     for copy in copies:
@@ -426,7 +433,7 @@
             + [pltpu.VMEM((groups, padded(p, 8), LANES), F32) for groups in (4, 4, 4, 3) for p in part]
             + [
                 pltpu.VMEM((num_dev, padded(rows, TILE), LANES), BF16), pltpu.VMEM(flat, F32),
-                pltpu.VMEM(flat, jnp.int32), pltpu.VMEM((num_dev, 8, LANES), F32),
+                pltpu.VMEM(flat, jnp.int32), pltpu.VMEM((num_dev, 1, LANES), F32),
                 dma((STAGES,)), dma((4,)),
                 dma((n, 4, 2, 3)), dma((n, 4, 2, 3)), dma((n, 4)), dma((n, 4)), dma((n, 3)), dma((n, 3)),
                 dma((num_dev - 1,)), dma((num_dev - 1,)),
@@ -442,7 +449,7 @@
             out_shape=(jax.ShapeDtypeStruct(whole, BF16), state, state, state, jax.ShapeDtypeStruct((1, LANES), F32)),
             in_specs=[vmem] * 5,
             out_specs=(hbm,) * 5,
-            scratch_shapes=[dma((5,))],
+            scratch_shapes=[dma((CHUNKS + 4,))],
             compiler_params=pltpu.CompilerParams(vmem_limit_bytes=1024 * 1024),
         )(*results)
         return (params.reshape(num_dev * shard_len), new_master.reshape(shard_len), new_first.reshape(shard_len),

time: 199 us -> 196 us (0.985)
  Pallas kernels: 197 us -> 194 us
    pallas_call x1, Pallas kernels: 191 us -> 188 us  [local_step(): pl.pallas_call(functools.partial(kernel, rows), out_shape=(pltpu.VMEM(who...]
where the time goes in v5:
time: 196 us; the launch traced here: 195 us
  Pallas kernels  194 us (99%)
    pallas_call x1, Pallas kernels, local_step(): pl.pallas_call(functools.partial(kernel, rows), out_shape=(pltpu.VMEM(who...  188 us
    pallas_call x1, Pallas kernels, local_step(): pl.pallas_call(write_out, out_shape=(jax.ShapeDtypeStruct(whole, BF16), s...  6.29 us

profile of v5, /device:TPU:0, one launch (start us, length us, event | category | flops | bytes accessed | tf_op | source)
XLA Modules:
  0.0 195.4 jit_solution(8590469315359783567)
XLA Ops:
  1.3 187.8 %shard_map.101 = (bf16[29376,2,128]{2,1,0:T(2,128)(2,1)S(1)}, f32[1836,128]{1,0:T(8,128)S(1)}, f32[1836,128]{1,0:T(8,128)S(1)}, f32[1836,128]{1,0:T(8,128)S(1)}, f32[1,128]{1,0:T(1,128)S(1)}) custom-call(bf16[1,7520256]{1,0:T(2,128)(2,1)} %grad_hbm.1, f32[1836,128]{1,0:T(8,128)} %bitcast.10, f32[1836,128]{1,0:T(8,128)} %bitcast.11, f32[1836,128]{1,0:T(8,128)} %bitcast.12, ...), custom_call_target="tpu_custom_call" | custom-call | tf_op jit(solution)/shard_map/pallas_call | solution.py:425
  189.1 6.3 %shard_map.102 = (bf16[29376,2,128]{2,1,0:T(2,128)(2,1)}, f32[1836,128]{1,0:T(8,128)}, f32[1836,128]{1,0:T(8,128)}, f32[1836,128]{1,0:T(8,128)}, f32[1,128]{1,0:T(1,128)}) custom-call(bf16[29376,2,128]{2,1,0:T(2,128)(2,1)S(1)} %get-tuple-element.15.refs_0_, f32[1836,128]{1,0:T(8,128)S(1)} %get-tuple-element.16.refs_1_, ...), custom_call_target="tpu_custom_call" | custom-call | tf_op jit(solution)/shard_map/pallas_call | solution.py:447

commit v6 on v5

--- a/solution.py
+++ b/solution.py
@@ -26,64 +26,63 @@
 REDUCE = (
     ((X, Y, LOW, HIGH), ((1, 1), (1, 0), (0, 1), (0, 0))),
     ((Y, X, LOW, HIGH), ((1, 1), (1, 0), (0, 1), (0, 0))),
-    ((LOW, HIGH, X, Y), ((1, 1), (1, 0), (0, 1), (0, 0))),
+    ((LOW, HIGH, X, Y), ((1, 1), (0, 1), (1, 0), (0, 0))),
 )
-REDUCE_TILES = (47, 47, 20)
+REDUCE_TILES = (46, 46, 22)
 SPAN_OF = (0, 0, 1)
 GATHER = (
     ((X, Y, LOW, HIGH), ((1, 1), (0, 1), (1, 0), (0, 0))),
     ((Y, X, LOW, HIGH), ((1, 1), (0, 1), (1, 0), (0, 0))),
-    ((LOW, HIGH, X, Y), ((1, 0), (1, 1), (0, 1), (0, 0))),
+    ((LOW, HIGH, X, Y), ((0, 1), (1, 1), (1, 0), (0, 0))),
 )
-GATHER_TILES = (48, 48, 18)
+GATHER_TILES = (49, 49, 16)
 REDUCE_ORDER = (
-    (0, 1, 0, 1, 1, 1), (0, 0, 0, 1, 1, 1), (1, 1, 0, 1, 2), (1, 0, 0, 1, 2), (0, 1, 0, 1, 1, 0), (1, 2, 0, 1, 1),
-    (0, 0, 0, 1, 1, 0), (0, 1, 0, 1, 0, 1), (1, 2, 0, 1, 2), (1, 1, 0, 1, 1), (1, 2, 0, 1, 0), (0, 0, 0, 1, 0, 1),
-    (0, 1, 0, 1, 0, 0), (0, 0, 0, 1, 0, 0), (0, 1, 0, 0, 1, 1), (0, 0, 0, 0, 1, 1), (0, 1, 0, 0, 1, 0),
-    (0, 0, 0, 0, 1, 0), (1, 0, 0, 0, 1), (0, 1, 0, 0, 0, 1), (0, 0, 0, 0, 0, 1), (0, 1, 0, 0, 0, 0),
-    (0, 0, 0, 0, 0, 0), (0, 1, 1, 1, 1, 1), (0, 0, 1, 1, 1, 1), (1, 2, 1, 1, 2), (0, 1, 1, 1, 1, 0),
-    (1, 2, 1, 1, 1), (0, 0, 1, 1, 1, 0), (0, 1, 1, 1, 0, 1), (0, 0, 1, 1, 0, 1), (0, 1, 1, 1, 0, 0),
-    (1, 0, 0, 1, 0), (0, 0, 1, 1, 0, 0), (0, 1, 1, 0, 1, 1), (2, 2, 0), (0, 0, 1, 0, 1, 1), (0, 1, 1, 0, 1, 0),
-    (1, 2, 0, 0, 2), (1, 1, 0, 0, 2), (0, 0, 1, 0, 1, 0), (0, 1, 1, 0, 0, 1), (0, 0, 1, 0, 0, 1), (1, 1, 0, 1, 0),
-    (1, 0, 0, 1, 1), (0, 1, 1, 0, 0, 0), (1, 1, 1, 1, 0), (0, 0, 1, 0, 0, 0), (0, 1, 2, 1, 1, 1),
-    (0, 0, 2, 1, 1, 1), (2, 1, 0), (3, 2, 0), (1, 2, 1, 1, 0), (1, 0, 0, 0, 2), (3, 1, 0), (0, 1, 2, 1, 1, 0),
-    (0, 0, 2, 1, 1, 0), (0, 1, 2, 1, 0, 1), (1, 2, 2, 1, 1), (1, 1, 0, 0, 1), (1, 2, 2, 1, 2), (0, 0, 2, 1, 0, 1),
-    (0, 1, 2, 1, 0, 0), (0, 0, 2, 1, 0, 0), (1, 1, 2, 0, 1), (1, 1, 1, 0, 0), (0, 1, 2, 0, 1, 1),
-    (0, 0, 2, 0, 1, 1), (0, 1, 2, 0, 1, 0), (2, 0, 0), (3, 0, 0), (1, 1, 2, 1, 0), (2, 2, 1), (1, 0, 0, 0, 0),
-    (1, 1, 1, 0, 2), (1, 2, 0, 0, 0), (1, 0, 2, 0, 2), (1, 1, 0, 0, 0), (0, 0, 2, 0, 1, 0), (1, 1, 2, 0, 2),
-    (0, 1, 2, 0, 0, 1), (0, 0, 2, 0, 0, 1), (0, 1, 2, 0, 0, 0), (0, 0, 2, 0, 0, 0), (1, 0, 1, 0, 0),
-    (0, 1, 3, 1, 1, 1), (3, 2, 1), (0, 0, 3, 1, 1, 1), (1, 0, 1, 1, 0), (1, 2, 2, 0, 0), (0, 1, 3, 1, 1, 0),
-    (1, 2, 3, 1, 1), (0, 0, 3, 1, 1, 0), (0, 1, 3, 1, 0, 1), (1, 0, 2, 0, 1), (1, 1, 1, 1, 1), (1, 2, 2, 1, 0),
-    (1, 1, 1, 1, 2), (1, 1, 2, 1, 1), (1, 1, 1, 0, 1), (2, 2, 2), (1, 0, 1, 1, 1), (1, 2, 2, 0, 2),
-    (0, 0, 3, 1, 0, 1), (1, 2, 3, 1, 0), (1, 1, 2, 0, 0), (0, 1, 3, 1, 0, 0), (1, 2, 1, 0, 2), (0, 0, 3, 1, 0, 0),
-    (1, 0, 1, 1, 2), (1, 2, 3, 1, 2), (1, 0, 2, 0, 0), (0, 1, 3, 0, 1, 1), (1, 0, 1, 0, 1), (0, 0, 3, 0, 1, 1),
-    (1, 2, 3, 0, 2), (1, 0, 1, 0, 2), (1, 1, 3, 1, 0), (0, 1, 3, 0, 1, 0), (1, 2, 3, 0, 1), (0, 0, 3, 0, 1, 0),
-    (0, 1, 3, 0, 0, 1), (1, 1, 2, 1, 2), (1, 2, 2, 0, 1), (1, 2, 0, 0, 1), (1, 0, 2, 1, 0), (1, 2, 1, 0, 0),
-    (1, 2, 1, 0, 1), (0, 0, 3, 0, 0, 1), (1, 1, 3, 0, 0), (1, 1, 3, 0, 1), (1, 0, 3, 0, 0), (1, 0, 2, 1, 1),
-    (4, 0, 0), (1, 1, 3, 0, 2), (4, 1, 0), (5, 1, 0), (6, 1, 0), (5, 0, 0), (6, 0, 0), (4, 2, 1), (5, 2, 1),
-    (1, 2, 3, 0, 0), (4, 2, 0), (2, 1, 1), (3, 1, 1), (1, 1, 3, 1, 1), (0, 1, 3, 0, 0, 0), (4, 2, 3),
-    (1, 0, 2, 1, 2), (2, 2, 3), (2, 1, 2), (3, 2, 2), (0, 0, 3, 0, 0, 0), (4, 0, 2), (1, 0, 3, 1, 0), (3, 1, 2),
-    (2, 0, 1), (5, 2, 0), (4, 2, 2), (1, 0, 3, 1, 1), (3, 2, 3), (1, 0, 3, 1, 2), (3, 0, 1), (1, 0, 3, 0, 1),
-    (4, 1, 1), (6, 2, 1), (5, 1, 1), (6, 1, 1), (4, 1, 2), (6, 2, 0), (2, 0, 2), (3, 0, 2), (5, 1, 2), (4, 1, 3),
-    (6, 1, 2), (4, 0, 1), (5, 0, 1), (6, 0, 1), (1, 1, 3, 1, 2), (5, 2, 2), (5, 0, 2), (6, 0, 2), (2, 0, 3),
-    (3, 0, 3), (1, 0, 3, 0, 2), (2, 1, 3), (3, 1, 3), (4, 0, 3), (5, 0, 3), (6, 2, 2), (5, 2, 3), (7, 2, 0),
-    (5, 1, 3), (7, 1, 0), (7, 0, 0),
+    (0, 1, 0, 1, 1, 1), (1, 2, 0, 1, 2), (0, 0, 0, 1, 1, 1), (0, 1, 0, 1, 1, 0), (0, 0, 0, 1, 1, 0),
+    (1, 1, 0, 1, 1), (1, 0, 0, 1, 1), (1, 2, 0, 1, 1), (0, 1, 0, 1, 0, 1), (0, 0, 0, 1, 0, 1), (0, 1, 0, 1, 0, 0),
+    (0, 0, 0, 1, 0, 0), (0, 1, 0, 0, 1, 1), (0, 0, 0, 0, 1, 1), (0, 1, 0, 0, 1, 0), (0, 0, 0, 0, 1, 0),
+    (0, 1, 0, 0, 0, 1), (1, 2, 0, 0, 2), (0, 0, 0, 0, 0, 1), (0, 1, 0, 0, 0, 0), (0, 0, 0, 0, 0, 0),
+    (0, 1, 1, 1, 1, 1), (1, 2, 1, 1, 2), (0, 0, 1, 1, 1, 1), (1, 1, 0, 1, 2), (0, 1, 1, 1, 1, 0), (1, 2, 1, 1, 1),
+    (0, 0, 1, 1, 1, 0), (0, 1, 1, 1, 0, 1), (0, 0, 1, 1, 0, 1), (1, 0, 0, 1, 2), (1, 2, 0, 1, 0), (1, 1, 0, 1, 0),
+    (0, 1, 1, 1, 0, 0), (0, 0, 1, 1, 0, 0), (1, 0, 0, 0, 0), (1, 1, 1, 1, 2), (0, 1, 1, 0, 1, 1),
+    (0, 0, 1, 0, 1, 1), (2, 2, 0), (3, 2, 0), (0, 1, 1, 0, 1, 0), (1, 2, 1, 0, 1), (0, 0, 1, 0, 1, 0),
+    (0, 1, 1, 0, 0, 1), (0, 0, 1, 0, 0, 1), (0, 1, 1, 0, 0, 0), (0, 0, 1, 0, 0, 0), (0, 1, 2, 1, 1, 1),
+    (0, 0, 2, 1, 1, 1), (0, 1, 2, 1, 1, 0), (1, 2, 2, 1, 1), (1, 0, 0, 0, 1), (0, 0, 2, 1, 1, 0), (1, 2, 2, 1, 2),
+    (0, 1, 2, 1, 0, 1), (1, 1, 0, 0, 1), (1, 1, 0, 0, 2), (0, 0, 2, 1, 0, 1), (0, 1, 2, 1, 0, 0), (2, 1, 0),
+    (0, 0, 2, 1, 0, 0), (1, 1, 2, 0, 1), (1, 2, 2, 1, 0), (0, 1, 2, 0, 1, 1), (1, 1, 0, 0, 0), (0, 0, 2, 0, 1, 1),
+    (0, 1, 2, 0, 1, 0), (0, 0, 2, 0, 1, 0), (0, 1, 2, 0, 0, 1), (1, 2, 1, 1, 0), (3, 1, 0), (2, 2, 1),
+    (0, 0, 2, 0, 0, 1), (1, 0, 0, 1, 0), (2, 0, 0), (0, 1, 2, 0, 0, 0), (0, 0, 2, 0, 0, 0), (3, 0, 0),
+    (1, 0, 0, 0, 2), (1, 0, 1, 1, 2), (1, 2, 0, 0, 0), (3, 2, 1), (1, 0, 2, 1, 0), (1, 2, 1, 0, 0), (1, 2, 2, 0, 1),
+    (1, 2, 0, 0, 1), (0, 1, 3, 1, 1, 1), (0, 0, 3, 1, 1, 1), (1, 2, 3, 1, 2), (1, 1, 2, 0, 0), (1, 2, 2, 0, 2),
+    (1, 1, 1, 1, 0), (0, 1, 3, 1, 1, 0), (0, 0, 3, 1, 1, 0), (0, 1, 3, 1, 0, 1), (0, 0, 3, 1, 0, 1),
+    (0, 1, 3, 1, 0, 0), (2, 2, 2), (1, 0, 2, 0, 2), (0, 0, 3, 1, 0, 0), (1, 1, 1, 0, 1), (0, 1, 3, 0, 1, 1),
+    (0, 0, 3, 0, 1, 1), (1, 0, 1, 1, 0), (1, 1, 1, 1, 1), (1, 2, 1, 0, 2), (1, 2, 3, 1, 0), (1, 1, 2, 0, 2),
+    (0, 1, 3, 0, 1, 0), (4, 1, 0), (0, 0, 3, 0, 1, 0), (1, 1, 1, 0, 2), (1, 1, 2, 1, 2), (1, 1, 2, 1, 1),
+    (1, 0, 2, 0, 1), (5, 1, 0), (1, 2, 3, 1, 1), (1, 0, 2, 0, 0), (1, 2, 3, 0, 2), (1, 2, 2, 0, 0), (1, 1, 2, 1, 0),
+    (1, 1, 3, 0, 2), (1, 2, 3, 0, 1), (1, 0, 1, 1, 1), (4, 0, 0), (6, 1, 0), (1, 1, 1, 0, 0), (1, 0, 1, 0, 1),
+    (5, 0, 0), (6, 0, 0), (0, 1, 3, 0, 0, 1), (0, 0, 3, 0, 0, 1), (1, 1, 3, 0, 0), (1, 0, 1, 0, 2), (4, 2, 1),
+    (1, 1, 3, 1, 0), (4, 2, 0), (5, 2, 0), (4, 1, 2), (2, 1, 1), (3, 1, 1), (0, 1, 3, 0, 0, 0), (0, 0, 3, 0, 0, 0),
+    (2, 1, 2), (3, 1, 2), (1, 0, 2, 1, 1), (3, 2, 2), (1, 0, 3, 0, 0), (6, 2, 0), (1, 0, 1, 0, 0), (1, 0, 3, 1, 0),
+    (2, 0, 1), (1, 0, 2, 1, 2), (1, 1, 3, 0, 1), (2, 2, 3), (3, 2, 3), (3, 0, 1), (4, 1, 1), (5, 1, 1), (6, 1, 1),
+    (5, 1, 2), (6, 1, 2), (1, 0, 3, 0, 1), (1, 0, 3, 0, 2), (4, 0, 1), (2, 0, 2), (3, 0, 2), (5, 0, 1), (4, 0, 2),
+    (5, 2, 1), (6, 0, 1), (1, 0, 3, 1, 1), (1, 1, 3, 1, 1), (1, 2, 3, 0, 0), (1, 0, 3, 1, 2), (4, 2, 2), (5, 2, 2),
+    (5, 0, 2), (4, 0, 3), (6, 0, 2), (1, 1, 3, 1, 2), (6, 2, 2), (2, 0, 3), (3, 0, 3), (4, 2, 3), (5, 2, 3),
+    (4, 1, 3), (2, 1, 3), (3, 1, 3), (6, 2, 1), (5, 1, 3), (7, 1, 0), (5, 0, 3), (7, 0, 0), (7, 2, 0),
 )
 GATHER_ORDER = (
-    (0, 2, 0), (1, 2, 1), (0, 0, 0), (3, 0, 3, 0), (1, 0, 2), (4, 2, 3, 0, 0), (1, 0, 0), (0, 1, 0), (2, 1, 3),
-    (2, 0, 3), (3, 1, 3, 0), (3, 0, 3, 1), (1, 1, 1), (1, 2, 2), (3, 1, 3, 1), (1, 1, 2), (3, 0, 2, 0),
-    (3, 0, 0, 0), (4, 0, 3, 0, 1), (1, 0, 1), (2, 0, 0), (2, 2, 2), (3, 1, 1, 0), (2, 1, 1), (2, 0, 2), (1, 2, 0),
-    (3, 1, 2, 0), (3, 2, 3, 0), (2, 1, 2), (4, 0, 1, 0, 0), (3, 2, 1, 0), (4, 1, 3, 0, 1), (1, 1, 0), (3, 0, 1, 0),
-    (4, 0, 0, 0, 1), (2, 0, 1), (4, 0, 0, 0, 0), (4, 2, 3, 0, 1), (3, 2, 2, 1), (4, 0, 3, 1, 0), (4, 1, 1, 1, 0),
-    (3, 1, 1, 1), (4, 0, 3, 0, 0), (3, 0, 0, 1), (4, 0, 2, 0, 1), (4, 2, 1, 0, 1), (4, 1, 3, 0, 0), (4, 0, 1, 1, 0),
-    (4, 2, 0, 0, 0), (4, 2, 2, 0, 0), (2, 2, 1), (4, 0, 2, 0, 0), (3, 2, 2, 0), (4, 2, 1, 0, 0), (2, 2, 3),
-    (3, 0, 1, 1), (2, 1, 0), (3, 1, 2, 1), (3, 2, 1, 1), (4, 1, 1, 0, 1), (4, 2, 2, 1, 1), (3, 0, 2, 1),
-    (4, 0, 1, 0, 1), (4, 1, 1, 1, 1), (2, 2, 0), (4, 0, 3, 1, 1), (4, 1, 2, 1, 0), (3, 2, 0, 0), (4, 0, 0, 1, 0),
-    (3, 1, 0, 0), (4, 0, 2, 1, 0), (4, 1, 3, 1, 1), (4, 1, 2, 1, 1), (4, 1, 3, 1, 0), (4, 2, 1, 1, 1),
-    (4, 0, 1, 1, 1), (3, 1, 0, 1), (4, 0, 0, 1, 1), (4, 2, 2, 0, 1), (4, 2, 1, 1, 0), (4, 1, 2, 0, 1),
-    (4, 1, 0, 0, 1), (4, 1, 2, 0, 0), (3, 2, 3, 1), (3, 2, 0, 1), (4, 2, 2, 1, 0), (4, 1, 0, 1, 0), (4, 2, 3, 1, 0),
-    (4, 1, 0, 0, 0), (4, 0, 2, 1, 1), (4, 1, 1, 0, 0), (4, 2, 0, 1, 0), (4, 2, 3, 1, 1), (4, 1, 0, 1, 1),
-    (4, 2, 0, 0, 1), (4, 2, 0, 1, 1),
+    (0, 2, 0), (1, 2, 1), (3, 2, 3, 0), (0, 0, 0), (1, 0, 2), (4, 2, 3, 0, 0), (1, 2, 0), (1, 0, 0), (2, 0, 3),
+    (0, 1, 0), (2, 1, 3), (3, 1, 3, 0), (3, 0, 2, 0), (2, 0, 2), (4, 0, 3, 1, 0), (3, 0, 3, 1), (1, 1, 2),
+    (1, 1, 0), (1, 2, 2), (3, 1, 3, 1), (4, 0, 2, 0, 0), (2, 2, 0), (3, 0, 0, 0), (2, 0, 0), (2, 1, 2),
+    (3, 1, 2, 0), (3, 2, 0, 1), (1, 1, 1), (2, 1, 0), (4, 0, 0, 0, 0), (4, 1, 3, 1, 0), (2, 2, 2), (3, 0, 2, 1),
+    (4, 1, 2, 1, 0), (3, 1, 0, 0), (3, 1, 2, 1), (4, 0, 0, 0, 1), (4, 1, 2, 0, 0), (3, 2, 0, 0), (1, 0, 1),
+    (3, 0, 0, 1), (3, 1, 1, 0), (4, 0, 3, 0, 0), (3, 2, 2, 1), (2, 1, 1), (3, 2, 1, 0), (4, 0, 2, 0, 1),
+    (3, 1, 0, 1), (4, 1, 1, 0, 0), (3, 0, 3, 0), (4, 0, 0, 1, 0), (4, 1, 1, 1, 0), (4, 2, 0, 1, 1), (2, 2, 3),
+    (4, 2, 1, 0, 0), (2, 0, 1), (4, 1, 3, 0, 1), (4, 0, 0, 1, 1), (4, 2, 0, 1, 0), (4, 2, 3, 0, 1), (4, 0, 1, 0, 0),
+    (2, 2, 1), (4, 2, 2, 1, 1), (4, 2, 2, 1, 0), (4, 1, 0, 0, 1), (4, 2, 2, 0, 0), (4, 0, 3, 1, 1), (4, 1, 3, 0, 0),
+    (4, 1, 0, 1, 0), (4, 1, 2, 0, 1), (4, 1, 1, 0, 1), (3, 1, 1, 1), (4, 1, 2, 1, 1), (4, 2, 0, 0, 1),
+    (4, 1, 0, 0, 0), (3, 0, 1, 0), (4, 1, 3, 1, 1), (4, 0, 2, 1, 0), (3, 2, 2, 0), (3, 0, 1, 1), (3, 2, 3, 1),
+    (4, 1, 0, 1, 1), (4, 0, 1, 0, 1), (4, 0, 2, 1, 1), (4, 0, 3, 0, 1), (3, 2, 1, 1), (4, 0, 1, 1, 0),
+    (4, 2, 3, 1, 1), (4, 1, 1, 1, 1), (4, 2, 1, 0, 1), (4, 2, 3, 1, 0), (4, 2, 1, 1, 0), (4, 2, 1, 1, 1),
+    (4, 2, 0, 0, 0), (4, 0, 1, 1, 1), (4, 2, 2, 0, 1),
 )
 HALF = ((1, 1), (1, 0), (0, 1), (0, 0))
 

time: 196 us -> 198 us (1.010)
  Pallas kernels: 194 us -> 196 us
where the time goes in v6:
time: 198 us; the launch traced here: 197 us
  Pallas kernels  196 us (99%)
    pallas_call x1, Pallas kernels, local_step(): pl.pallas_call(functools.partial(kernel, rows), out_shape=(pltpu.VMEM(who...  190 us
    pallas_call x1, Pallas kernels, local_step(): pl.pallas_call(write_out, out_shape=(jax.ShapeDtypeStruct(whole, BF16), s...  6.29 us

profile of v6, /device:TPU:0, one launch (start us, length us, event | category | flops | bytes accessed | tf_op | source)
XLA Modules:
  0.0 197.2 jit_solution(8673189605872836006)
XLA Ops:
  1.3 189.6 %shard_map.101 = (bf16[29376,2,128]{2,1,0:T(2,128)(2,1)S(1)}, f32[1836,128]{1,0:T(8,128)S(1)}, f32[1836,128]{1,0:T(8,128)S(1)}, f32[1836,128]{1,0:T(8,128)S(1)}, f32[1,128]{1,0:T(1,128)S(1)}) custom-call(bf16[1,7520256]{1,0:T(2,128)(2,1)} %grad_hbm.1, f32[1836,128]{1,0:T(8,128)} %bitcast.10, f32[1836,128]{1,0:T(8,128)} %bitcast.11, f32[1836,128]{1,0:T(8,128)} %bitcast.12, ...), custom_call_target="tpu_custom_call" | custom-call | tf_op jit(solution)/shard_map/pallas_call | solution.py:424
  190.9 6.3 %shard_map.102 = (bf16[29376,2,128]{2,1,0:T(2,128)(2,1)}, f32[1836,128]{1,0:T(8,128)}, f32[1836,128]{1,0:T(8,128)}, f32[1836,128]{1,0:T(8,128)}, f32[1,128]{1,0:T(1,128)}) custom-call(bf16[29376,2,128]{2,1,0:T(2,128)(2,1)S(1)} %get-tuple-element.15.refs_0_, f32[1836,128]{1,0:T(8,128)S(1)} %get-tuple-element.16.refs_1_, ...), custom_call_target="tpu_custom_call" | custom-call | tf_op jit(solution)/shard_map/pallas_call | solution.py:446

commit v7 on v6

--- a/solution.py
+++ b/solution.py
@@ -28,7 +28,7 @@
     ((Y, X, LOW, HIGH), ((1, 1), (1, 0), (0, 1), (0, 0))),
     ((LOW, HIGH, X, Y), ((1, 1), (0, 1), (1, 0), (0, 0))),
 )
-REDUCE_TILES = (46, 46, 22)
+REDUCE_TILES = (47, 47, 20)
 SPAN_OF = (0, 0, 1)
 GATHER = (
     ((X, Y, LOW, HIGH), ((1, 1), (0, 1), (1, 0), (0, 0))),
@@ -37,52 +37,53 @@
 )
 GATHER_TILES = (49, 49, 16)
 REDUCE_ORDER = (
-    (0, 1, 0, 1, 1, 1), (1, 2, 0, 1, 2), (0, 0, 0, 1, 1, 1), (0, 1, 0, 1, 1, 0), (0, 0, 0, 1, 1, 0),
-    (1, 1, 0, 1, 1), (1, 0, 0, 1, 1), (1, 2, 0, 1, 1), (0, 1, 0, 1, 0, 1), (0, 0, 0, 1, 0, 1), (0, 1, 0, 1, 0, 0),
-    (0, 0, 0, 1, 0, 0), (0, 1, 0, 0, 1, 1), (0, 0, 0, 0, 1, 1), (0, 1, 0, 0, 1, 0), (0, 0, 0, 0, 1, 0),
-    (0, 1, 0, 0, 0, 1), (1, 2, 0, 0, 2), (0, 0, 0, 0, 0, 1), (0, 1, 0, 0, 0, 0), (0, 0, 0, 0, 0, 0),
-    (0, 1, 1, 1, 1, 1), (1, 2, 1, 1, 2), (0, 0, 1, 1, 1, 1), (1, 1, 0, 1, 2), (0, 1, 1, 1, 1, 0), (1, 2, 1, 1, 1),
-    (0, 0, 1, 1, 1, 0), (0, 1, 1, 1, 0, 1), (0, 0, 1, 1, 0, 1), (1, 0, 0, 1, 2), (1, 2, 0, 1, 0), (1, 1, 0, 1, 0),
-    (0, 1, 1, 1, 0, 0), (0, 0, 1, 1, 0, 0), (1, 0, 0, 0, 0), (1, 1, 1, 1, 2), (0, 1, 1, 0, 1, 1),
-    (0, 0, 1, 0, 1, 1), (2, 2, 0), (3, 2, 0), (0, 1, 1, 0, 1, 0), (1, 2, 1, 0, 1), (0, 0, 1, 0, 1, 0),
-    (0, 1, 1, 0, 0, 1), (0, 0, 1, 0, 0, 1), (0, 1, 1, 0, 0, 0), (0, 0, 1, 0, 0, 0), (0, 1, 2, 1, 1, 1),
-    (0, 0, 2, 1, 1, 1), (0, 1, 2, 1, 1, 0), (1, 2, 2, 1, 1), (1, 0, 0, 0, 1), (0, 0, 2, 1, 1, 0), (1, 2, 2, 1, 2),
-    (0, 1, 2, 1, 0, 1), (1, 1, 0, 0, 1), (1, 1, 0, 0, 2), (0, 0, 2, 1, 0, 1), (0, 1, 2, 1, 0, 0), (2, 1, 0),
-    (0, 0, 2, 1, 0, 0), (1, 1, 2, 0, 1), (1, 2, 2, 1, 0), (0, 1, 2, 0, 1, 1), (1, 1, 0, 0, 0), (0, 0, 2, 0, 1, 1),
-    (0, 1, 2, 0, 1, 0), (0, 0, 2, 0, 1, 0), (0, 1, 2, 0, 0, 1), (1, 2, 1, 1, 0), (3, 1, 0), (2, 2, 1),
-    (0, 0, 2, 0, 0, 1), (1, 0, 0, 1, 0), (2, 0, 0), (0, 1, 2, 0, 0, 0), (0, 0, 2, 0, 0, 0), (3, 0, 0),
-    (1, 0, 0, 0, 2), (1, 0, 1, 1, 2), (1, 2, 0, 0, 0), (3, 2, 1), (1, 0, 2, 1, 0), (1, 2, 1, 0, 0), (1, 2, 2, 0, 1),
-    (1, 2, 0, 0, 1), (0, 1, 3, 1, 1, 1), (0, 0, 3, 1, 1, 1), (1, 2, 3, 1, 2), (1, 1, 2, 0, 0), (1, 2, 2, 0, 2),
-    (1, 1, 1, 1, 0), (0, 1, 3, 1, 1, 0), (0, 0, 3, 1, 1, 0), (0, 1, 3, 1, 0, 1), (0, 0, 3, 1, 0, 1),
-    (0, 1, 3, 1, 0, 0), (2, 2, 2), (1, 0, 2, 0, 2), (0, 0, 3, 1, 0, 0), (1, 1, 1, 0, 1), (0, 1, 3, 0, 1, 1),
-    (0, 0, 3, 0, 1, 1), (1, 0, 1, 1, 0), (1, 1, 1, 1, 1), (1, 2, 1, 0, 2), (1, 2, 3, 1, 0), (1, 1, 2, 0, 2),
-    (0, 1, 3, 0, 1, 0), (4, 1, 0), (0, 0, 3, 0, 1, 0), (1, 1, 1, 0, 2), (1, 1, 2, 1, 2), (1, 1, 2, 1, 1),
-    (1, 0, 2, 0, 1), (5, 1, 0), (1, 2, 3, 1, 1), (1, 0, 2, 0, 0), (1, 2, 3, 0, 2), (1, 2, 2, 0, 0), (1, 1, 2, 1, 0),
-    (1, 1, 3, 0, 2), (1, 2, 3, 0, 1), (1, 0, 1, 1, 1), (4, 0, 0), (6, 1, 0), (1, 1, 1, 0, 0), (1, 0, 1, 0, 1),
-    (5, 0, 0), (6, 0, 0), (0, 1, 3, 0, 0, 1), (0, 0, 3, 0, 0, 1), (1, 1, 3, 0, 0), (1, 0, 1, 0, 2), (4, 2, 1),
-    (1, 1, 3, 1, 0), (4, 2, 0), (5, 2, 0), (4, 1, 2), (2, 1, 1), (3, 1, 1), (0, 1, 3, 0, 0, 0), (0, 0, 3, 0, 0, 0),
-    (2, 1, 2), (3, 1, 2), (1, 0, 2, 1, 1), (3, 2, 2), (1, 0, 3, 0, 0), (6, 2, 0), (1, 0, 1, 0, 0), (1, 0, 3, 1, 0),
-    (2, 0, 1), (1, 0, 2, 1, 2), (1, 1, 3, 0, 1), (2, 2, 3), (3, 2, 3), (3, 0, 1), (4, 1, 1), (5, 1, 1), (6, 1, 1),
-    (5, 1, 2), (6, 1, 2), (1, 0, 3, 0, 1), (1, 0, 3, 0, 2), (4, 0, 1), (2, 0, 2), (3, 0, 2), (5, 0, 1), (4, 0, 2),
-    (5, 2, 1), (6, 0, 1), (1, 0, 3, 1, 1), (1, 1, 3, 1, 1), (1, 2, 3, 0, 0), (1, 0, 3, 1, 2), (4, 2, 2), (5, 2, 2),
-    (5, 0, 2), (4, 0, 3), (6, 0, 2), (1, 1, 3, 1, 2), (6, 2, 2), (2, 0, 3), (3, 0, 3), (4, 2, 3), (5, 2, 3),
-    (4, 1, 3), (2, 1, 3), (3, 1, 3), (6, 2, 1), (5, 1, 3), (7, 1, 0), (5, 0, 3), (7, 0, 0), (7, 2, 0),
+    (0, 1, 0, 1, 1, 1), (0, 0, 0, 1, 1, 1), (1, 0, 0, 1, 2), (0, 1, 0, 1, 1, 0), (1, 2, 0, 1, 1), (1, 1, 0, 1, 2),
+    (0, 0, 0, 1, 1, 0), (1, 1, 0, 1, 1), (1, 0, 0, 1, 1), (0, 1, 0, 1, 0, 1), (1, 2, 0, 1, 0), (0, 0, 0, 1, 0, 1),
+    (1, 0, 0, 1, 0), (0, 1, 0, 1, 0, 0), (0, 0, 0, 1, 0, 0), (0, 1, 0, 0, 1, 1), (0, 0, 0, 0, 1, 1),
+    (0, 1, 0, 0, 1, 0), (0, 0, 0, 0, 1, 0), (0, 1, 0, 0, 0, 1), (0, 0, 0, 0, 0, 1), (0, 1, 0, 0, 0, 0),
+    (1, 0, 0, 0, 2), (0, 0, 0, 0, 0, 0), (0, 1, 1, 1, 1, 1), (1, 2, 0, 1, 2), (1, 1, 0, 1, 0), (1, 0, 0, 0, 0),
+    (0, 0, 1, 1, 1, 1), (1, 2, 1, 1, 2), (1, 1, 0, 0, 2), (0, 1, 1, 1, 1, 0), (0, 0, 1, 1, 1, 0),
+    (0, 1, 1, 1, 0, 1), (0, 0, 1, 1, 0, 1), (0, 1, 1, 1, 0, 0), (0, 0, 1, 1, 0, 0), (0, 1, 1, 0, 1, 1),
+    (1, 1, 1, 0, 1), (0, 0, 1, 0, 1, 1), (0, 1, 1, 0, 1, 0), (1, 1, 1, 1, 1), (0, 0, 1, 0, 1, 0),
+    (0, 1, 1, 0, 0, 1), (0, 0, 1, 0, 0, 1), (1, 1, 1, 0, 0), (0, 1, 1, 0, 0, 0), (0, 0, 1, 0, 0, 0),
+    (0, 1, 2, 1, 1, 1), (0, 0, 2, 1, 1, 1), (0, 1, 2, 1, 1, 0), (1, 2, 1, 1, 1), (1, 0, 0, 0, 1), (2, 2, 0),
+    (3, 2, 0), (0, 0, 2, 1, 1, 0), (1, 2, 1, 1, 0), (1, 1, 0, 0, 1), (0, 1, 2, 1, 0, 1), (0, 0, 2, 1, 0, 1),
+    (0, 1, 2, 1, 0, 0), (0, 0, 2, 1, 0, 0), (2, 0, 0), (3, 0, 0), (0, 1, 2, 0, 1, 1), (1, 2, 2, 1, 1),
+    (1, 0, 1, 1, 0), (0, 0, 2, 0, 1, 1), (0, 1, 2, 0, 1, 0), (2, 1, 0), (2, 2, 1), (3, 1, 0), (1, 2, 2, 0, 1),
+    (0, 0, 2, 0, 1, 0), (0, 1, 2, 0, 0, 1), (1, 2, 2, 0, 0), (0, 0, 2, 0, 0, 1), (1, 0, 2, 0, 0),
+    (0, 1, 2, 0, 0, 0), (1, 1, 2, 0, 1), (1, 2, 0, 0, 2), (1, 1, 1, 0, 2), (0, 0, 2, 0, 0, 0), (0, 1, 3, 1, 1, 1),
+    (1, 0, 2, 1, 1), (1, 0, 2, 0, 2), (1, 2, 2, 1, 0), (1, 2, 1, 0, 0), (0, 0, 3, 1, 1, 1), (0, 1, 3, 1, 1, 0),
+    (1, 0, 2, 1, 2), (3, 2, 1), (1, 2, 2, 0, 2), (0, 0, 3, 1, 1, 0), (0, 1, 3, 1, 0, 1), (1, 1, 2, 0, 0),
+    (1, 2, 3, 1, 2), (0, 0, 3, 1, 0, 1), (1, 1, 3, 0, 2), (1, 2, 2, 1, 2), (1, 0, 1, 1, 1), (0, 1, 3, 1, 0, 0),
+    (0, 0, 3, 1, 0, 0), (4, 0, 0), (1, 2, 1, 0, 1), (1, 2, 1, 0, 2), (0, 1, 3, 0, 1, 1), (0, 0, 3, 0, 1, 1),
+    (1, 2, 0, 0, 1), (0, 1, 3, 0, 1, 0), (0, 0, 3, 0, 1, 0), (1, 2, 3, 0, 1), (1, 2, 3, 1, 1), (1, 1, 0, 0, 0),
+    (1, 0, 1, 0, 1), (0, 1, 3, 0, 0, 1), (1, 0, 3, 1, 0), (1, 1, 1, 1, 0), (4, 1, 0), (1, 2, 3, 0, 2),
+    (0, 0, 3, 0, 0, 1), (1, 0, 3, 0, 0), (0, 1, 3, 0, 0, 0), (1, 1, 1, 1, 2), (5, 1, 0), (6, 1, 0), (5, 0, 0),
+    (1, 0, 2, 1, 0), (1, 0, 1, 1, 2), (1, 1, 2, 1, 2), (1, 0, 2, 0, 1), (6, 0, 0), (1, 0, 1, 0, 2), (1, 1, 2, 1, 1),
+    (2, 2, 2), (3, 2, 2), (1, 1, 2, 1, 0), (2, 1, 1), (3, 1, 1), (0, 0, 3, 0, 0, 0), (1, 2, 3, 1, 0),
+    (1, 1, 3, 0, 1), (1, 1, 3, 1, 0), (1, 1, 3, 1, 1), (1, 1, 2, 0, 2), (2, 1, 2), (1, 0, 1, 0, 0), (3, 1, 2),
+    (4, 2, 1), (5, 2, 1), (6, 2, 1), (2, 2, 3), (3, 2, 3), (4, 2, 2), (1, 2, 3, 0, 0), (2, 0, 1), (1, 0, 3, 1, 1),
+    (3, 0, 1), (1, 1, 3, 0, 0), (4, 1, 1), (5, 1, 1), (6, 1, 1), (5, 2, 2), (6, 2, 2), (1, 2, 0, 0, 0), (4, 1, 2),
+    (5, 1, 2), (6, 1, 2), (1, 0, 3, 0, 1), (4, 2, 0), (1, 0, 3, 1, 2), (2, 0, 2), (3, 0, 2), (1, 1, 3, 1, 2),
+    (4, 0, 1), (5, 0, 1), (6, 0, 1), (5, 2, 0), (6, 2, 0), (1, 0, 3, 0, 2), (2, 0, 3), (4, 0, 2), (3, 0, 3),
+    (5, 0, 2), (6, 0, 2), (4, 2, 3), (5, 2, 3), (2, 1, 3), (3, 1, 3), (4, 1, 3), (5, 1, 3), (7, 1, 0), (7, 2, 0),
+    (4, 0, 3), (5, 0, 3), (7, 0, 0),
 )
 GATHER_ORDER = (
-    (0, 2, 0), (1, 2, 1), (3, 2, 3, 0), (0, 0, 0), (1, 0, 2), (4, 2, 3, 0, 0), (1, 2, 0), (1, 0, 0), (2, 0, 3),
-    (0, 1, 0), (2, 1, 3), (3, 1, 3, 0), (3, 0, 2, 0), (2, 0, 2), (4, 0, 3, 1, 0), (3, 0, 3, 1), (1, 1, 2),
-    (1, 1, 0), (1, 2, 2), (3, 1, 3, 1), (4, 0, 2, 0, 0), (2, 2, 0), (3, 0, 0, 0), (2, 0, 0), (2, 1, 2),
-    (3, 1, 2, 0), (3, 2, 0, 1), (1, 1, 1), (2, 1, 0), (4, 0, 0, 0, 0), (4, 1, 3, 1, 0), (2, 2, 2), (3, 0, 2, 1),
-    (4, 1, 2, 1, 0), (3, 1, 0, 0), (3, 1, 2, 1), (4, 0, 0, 0, 1), (4, 1, 2, 0, 0), (3, 2, 0, 0), (1, 0, 1),
-    (3, 0, 0, 1), (3, 1, 1, 0), (4, 0, 3, 0, 0), (3, 2, 2, 1), (2, 1, 1), (3, 2, 1, 0), (4, 0, 2, 0, 1),
-    (3, 1, 0, 1), (4, 1, 1, 0, 0), (3, 0, 3, 0), (4, 0, 0, 1, 0), (4, 1, 1, 1, 0), (4, 2, 0, 1, 1), (2, 2, 3),
-    (4, 2, 1, 0, 0), (2, 0, 1), (4, 1, 3, 0, 1), (4, 0, 0, 1, 1), (4, 2, 0, 1, 0), (4, 2, 3, 0, 1), (4, 0, 1, 0, 0),
-    (2, 2, 1), (4, 2, 2, 1, 1), (4, 2, 2, 1, 0), (4, 1, 0, 0, 1), (4, 2, 2, 0, 0), (4, 0, 3, 1, 1), (4, 1, 3, 0, 0),
-    (4, 1, 0, 1, 0), (4, 1, 2, 0, 1), (4, 1, 1, 0, 1), (3, 1, 1, 1), (4, 1, 2, 1, 1), (4, 2, 0, 0, 1),
-    (4, 1, 0, 0, 0), (3, 0, 1, 0), (4, 1, 3, 1, 1), (4, 0, 2, 1, 0), (3, 2, 2, 0), (3, 0, 1, 1), (3, 2, 3, 1),
-    (4, 1, 0, 1, 1), (4, 0, 1, 0, 1), (4, 0, 2, 1, 1), (4, 0, 3, 0, 1), (3, 2, 1, 1), (4, 0, 1, 1, 0),
-    (4, 2, 3, 1, 1), (4, 1, 1, 1, 1), (4, 2, 1, 0, 1), (4, 2, 3, 1, 0), (4, 2, 1, 1, 0), (4, 2, 1, 1, 1),
-    (4, 2, 0, 0, 0), (4, 0, 1, 1, 1), (4, 2, 2, 0, 1),
+    (0, 2, 0), (1, 2, 1), (3, 2, 3, 0), (1, 2, 0), (0, 0, 0), (1, 0, 2), (2, 0, 3), (1, 2, 2), (1, 0, 0), (0, 1, 0),
+    (4, 1, 3, 0, 0), (2, 1, 3), (2, 0, 2), (3, 0, 2, 0), (4, 0, 3, 1, 0), (2, 2, 2), (3, 1, 3, 1), (3, 0, 3, 1),
+    (2, 0, 0), (4, 2, 3, 0, 1), (3, 1, 3, 0), (4, 0, 2, 1, 0), (1, 1, 2), (1, 1, 0), (2, 2, 0), (3, 0, 2, 1),
+    (3, 0, 0, 0), (3, 1, 2, 0), (4, 1, 3, 1, 1), (4, 2, 2, 0, 0), (2, 1, 2), (3, 2, 0, 1), (1, 1, 1), (3, 1, 0, 0),
+    (2, 1, 0), (4, 1, 0, 0, 0), (1, 0, 1), (4, 0, 3, 0, 0), (4, 0, 0, 0, 1), (4, 2, 1, 0, 0), (3, 1, 2, 1),
+    (3, 2, 2, 0), (3, 2, 0, 0), (4, 0, 2, 1, 1), (4, 2, 0, 1, 0), (4, 1, 3, 1, 0), (2, 2, 1), (4, 1, 2, 1, 0),
+    (4, 0, 0, 0, 0), (3, 0, 0, 1), (3, 1, 0, 1), (2, 2, 3), (3, 0, 3, 0), (3, 2, 2, 1), (4, 1, 2, 1, 1),
+    (4, 1, 3, 0, 1), (2, 1, 1), (4, 0, 0, 1, 0), (4, 0, 0, 1, 1), (4, 0, 2, 0, 0), (3, 1, 1, 0), (3, 2, 1, 0),
+    (4, 2, 2, 1, 0), (2, 0, 1), (4, 1, 1, 0, 0), (4, 0, 3, 0, 1), (3, 0, 1, 0), (4, 2, 0, 0, 0), (4, 1, 2, 0, 0),
+    (4, 1, 1, 0, 1), (3, 1, 1, 1), (4, 1, 1, 1, 0), (4, 1, 0, 1, 1), (4, 2, 2, 0, 1), (4, 2, 3, 1, 0),
+    (4, 1, 2, 0, 1), (4, 0, 3, 1, 1), (3, 0, 1, 1), (4, 0, 1, 1, 0), (4, 2, 0, 0, 1), (4, 0, 2, 0, 1),
+    (4, 2, 0, 1, 1), (4, 2, 2, 1, 1), (4, 1, 0, 0, 1), (3, 2, 3, 1), (4, 2, 1, 0, 1), (4, 2, 1, 1, 0),
+    (4, 1, 0, 1, 0), (3, 2, 1, 1), (4, 2, 3, 0, 0), (4, 0, 1, 0, 1), (4, 0, 1, 0, 0), (4, 1, 1, 1, 1),
+    (4, 2, 3, 1, 1), (4, 2, 1, 1, 1), (4, 0, 1, 1, 1),
 )
 HALF = ((1, 1), (1, 0), (0, 1), (0, 0))
 

time: 198 us -> 196 us (0.990)
  Pallas kernels: 196 us -> 194 us
where the time goes in v7:
time: 196 us
  Pallas kernels  194 us (99%)
    pallas_call x1, Pallas kernels, local_step(): pl.pallas_call(functools.partial(kernel, rows), out_shape=(pltpu.VMEM(who...  188 us
    pallas_call x1, Pallas kernels, local_step(): pl.pallas_call(write_out, out_shape=(jax.ShapeDtypeStruct(whole, BF16), s...  6.29 us

profile of v7, /device:TPU:0, one launch (start us, length us, event | category | flops | bytes accessed | tf_op | source)
XLA Modules:
  0.0 195.6 jit_solution(9697348376587090428)
XLA Ops:
  1.3 188.0 %shard_map.101 = (bf16[29376,2,128]{2,1,0:T(2,128)(2,1)S(1)}, f32[1836,128]{1,0:T(8,128)S(1)}, f32[1836,128]{1,0:T(8,128)S(1)}, f32[1836,128]{1,0:T(8,128)S(1)}, f32[1,128]{1,0:T(1,128)S(1)}) custom-call(bf16[1,7520256]{1,0:T(2,128)(2,1)} %grad_hbm.1, f32[1836,128]{1,0:T(8,128)} %bitcast.10, f32[1836,128]{1,0:T(8,128)} %bitcast.11, f32[1836,128]{1,0:T(8,128)} %bitcast.12, ...), custom_call_target="tpu_custom_call" | custom-call | tf_op jit(solution)/shard_map/pallas_call | solution.py:425
  189.3 6.3 %shard_map.102 = (bf16[29376,2,128]{2,1,0:T(2,128)(2,1)}, f32[1836,128]{1,0:T(8,128)}, f32[1836,128]{1,0:T(8,128)}, f32[1836,128]{1,0:T(8,128)}, f32[1,128]{1,0:T(1,128)}) custom-call(bf16[29376,2,128]{2,1,0:T(2,128)(2,1)S(1)} %get-tuple-element.15.refs_0_, f32[1836,128]{1,0:T(8,128)S(1)} %get-tuple-element.16.refs_1_, ...), custom_call_target="tpu_custom_call" | custom-call | tf_op jit(solution)/shard_map/pallas_call | solution.py:447

commit v8 on v5

--- a/solution.py
+++ b/solution.py
@@ -26,7 +26,7 @@
 REDUCE = (
     ((X, Y, LOW, HIGH), ((1, 1), (1, 0), (0, 1), (0, 0))),
     ((Y, X, LOW, HIGH), ((1, 1), (1, 0), (0, 1), (0, 0))),
-    ((LOW, HIGH, X, Y), ((1, 1), (1, 0), (0, 1), (0, 0))),
+    ((LOW, HIGH, X, Y), ((1, 1), (0, 1), (1, 0), (0, 0))),
 )
 REDUCE_TILES = (47, 47, 20)
 SPAN_OF = (0, 0, 1)
@@ -37,37 +37,37 @@
 )
 GATHER_TILES = (48, 48, 18)
 REDUCE_ORDER = (
-    (0, 1, 0, 1, 1, 1), (0, 0, 0, 1, 1, 1), (1, 1, 0, 1, 2), (1, 0, 0, 1, 2), (0, 1, 0, 1, 1, 0), (1, 2, 0, 1, 1),
-    (0, 0, 0, 1, 1, 0), (0, 1, 0, 1, 0, 1), (1, 2, 0, 1, 2), (1, 1, 0, 1, 1), (1, 2, 0, 1, 0), (0, 0, 0, 1, 0, 1),
+    (0, 1, 0, 1, 1, 1), (0, 0, 0, 1, 1, 1), (1, 0, 0, 1, 2), (0, 1, 0, 1, 1, 0), (1, 2, 0, 1, 1), (1, 1, 0, 1, 2),
+    (0, 0, 0, 1, 1, 0), (1, 0, 0, 1, 1), (1, 1, 0, 1, 1), (0, 1, 0, 1, 0, 1), (0, 0, 0, 1, 0, 1),
     (0, 1, 0, 1, 0, 0), (0, 0, 0, 1, 0, 0), (0, 1, 0, 0, 1, 1), (0, 0, 0, 0, 1, 1), (0, 1, 0, 0, 1, 0),
-    (0, 0, 0, 0, 1, 0), (1, 0, 0, 0, 1), (0, 1, 0, 0, 0, 1), (0, 0, 0, 0, 0, 1), (0, 1, 0, 0, 0, 0),
-    (0, 0, 0, 0, 0, 0), (0, 1, 1, 1, 1, 1), (0, 0, 1, 1, 1, 1), (1, 2, 1, 1, 2), (0, 1, 1, 1, 1, 0),
-    (1, 2, 1, 1, 1), (0, 0, 1, 1, 1, 0), (0, 1, 1, 1, 0, 1), (0, 0, 1, 1, 0, 1), (0, 1, 1, 1, 0, 0),
-    (1, 0, 0, 1, 0), (0, 0, 1, 1, 0, 0), (0, 1, 1, 0, 1, 1), (2, 2, 0), (0, 0, 1, 0, 1, 1), (0, 1, 1, 0, 1, 0),
-    (1, 2, 0, 0, 2), (1, 1, 0, 0, 2), (0, 0, 1, 0, 1, 0), (0, 1, 1, 0, 0, 1), (0, 0, 1, 0, 0, 1), (1, 1, 0, 1, 0),
-    (1, 0, 0, 1, 1), (0, 1, 1, 0, 0, 0), (1, 1, 1, 1, 0), (0, 0, 1, 0, 0, 0), (0, 1, 2, 1, 1, 1),
-    (0, 0, 2, 1, 1, 1), (2, 1, 0), (3, 2, 0), (1, 2, 1, 1, 0), (1, 0, 0, 0, 2), (3, 1, 0), (0, 1, 2, 1, 1, 0),
-    (0, 0, 2, 1, 1, 0), (0, 1, 2, 1, 0, 1), (1, 2, 2, 1, 1), (1, 1, 0, 0, 1), (1, 2, 2, 1, 2), (0, 0, 2, 1, 0, 1),
-    (0, 1, 2, 1, 0, 0), (0, 0, 2, 1, 0, 0), (1, 1, 2, 0, 1), (1, 1, 1, 0, 0), (0, 1, 2, 0, 1, 1),
-    (0, 0, 2, 0, 1, 1), (0, 1, 2, 0, 1, 0), (2, 0, 0), (3, 0, 0), (1, 1, 2, 1, 0), (2, 2, 1), (1, 0, 0, 0, 0),
-    (1, 1, 1, 0, 2), (1, 2, 0, 0, 0), (1, 0, 2, 0, 2), (1, 1, 0, 0, 0), (0, 0, 2, 0, 1, 0), (1, 1, 2, 0, 2),
-    (0, 1, 2, 0, 0, 1), (0, 0, 2, 0, 0, 1), (0, 1, 2, 0, 0, 0), (0, 0, 2, 0, 0, 0), (1, 0, 1, 0, 0),
-    (0, 1, 3, 1, 1, 1), (3, 2, 1), (0, 0, 3, 1, 1, 1), (1, 0, 1, 1, 0), (1, 2, 2, 0, 0), (0, 1, 3, 1, 1, 0),
-    (1, 2, 3, 1, 1), (0, 0, 3, 1, 1, 0), (0, 1, 3, 1, 0, 1), (1, 0, 2, 0, 1), (1, 1, 1, 1, 1), (1, 2, 2, 1, 0),
-    (1, 1, 1, 1, 2), (1, 1, 2, 1, 1), (1, 1, 1, 0, 1), (2, 2, 2), (1, 0, 1, 1, 1), (1, 2, 2, 0, 2),
-    (0, 0, 3, 1, 0, 1), (1, 2, 3, 1, 0), (1, 1, 2, 0, 0), (0, 1, 3, 1, 0, 0), (1, 2, 1, 0, 2), (0, 0, 3, 1, 0, 0),
-    (1, 0, 1, 1, 2), (1, 2, 3, 1, 2), (1, 0, 2, 0, 0), (0, 1, 3, 0, 1, 1), (1, 0, 1, 0, 1), (0, 0, 3, 0, 1, 1),
-    (1, 2, 3, 0, 2), (1, 0, 1, 0, 2), (1, 1, 3, 1, 0), (0, 1, 3, 0, 1, 0), (1, 2, 3, 0, 1), (0, 0, 3, 0, 1, 0),
-    (0, 1, 3, 0, 0, 1), (1, 1, 2, 1, 2), (1, 2, 2, 0, 1), (1, 2, 0, 0, 1), (1, 0, 2, 1, 0), (1, 2, 1, 0, 0),
-    (1, 2, 1, 0, 1), (0, 0, 3, 0, 0, 1), (1, 1, 3, 0, 0), (1, 1, 3, 0, 1), (1, 0, 3, 0, 0), (1, 0, 2, 1, 1),
-    (4, 0, 0), (1, 1, 3, 0, 2), (4, 1, 0), (5, 1, 0), (6, 1, 0), (5, 0, 0), (6, 0, 0), (4, 2, 1), (5, 2, 1),
-    (1, 2, 3, 0, 0), (4, 2, 0), (2, 1, 1), (3, 1, 1), (1, 1, 3, 1, 1), (0, 1, 3, 0, 0, 0), (4, 2, 3),
-    (1, 0, 2, 1, 2), (2, 2, 3), (2, 1, 2), (3, 2, 2), (0, 0, 3, 0, 0, 0), (4, 0, 2), (1, 0, 3, 1, 0), (3, 1, 2),
-    (2, 0, 1), (5, 2, 0), (4, 2, 2), (1, 0, 3, 1, 1), (3, 2, 3), (1, 0, 3, 1, 2), (3, 0, 1), (1, 0, 3, 0, 1),
-    (4, 1, 1), (6, 2, 1), (5, 1, 1), (6, 1, 1), (4, 1, 2), (6, 2, 0), (2, 0, 2), (3, 0, 2), (5, 1, 2), (4, 1, 3),
-    (6, 1, 2), (4, 0, 1), (5, 0, 1), (6, 0, 1), (1, 1, 3, 1, 2), (5, 2, 2), (5, 0, 2), (6, 0, 2), (2, 0, 3),
-    (3, 0, 3), (1, 0, 3, 0, 2), (2, 1, 3), (3, 1, 3), (4, 0, 3), (5, 0, 3), (6, 2, 2), (5, 2, 3), (7, 2, 0),
-    (5, 1, 3), (7, 1, 0), (7, 0, 0),
+    (0, 0, 0, 0, 1, 0), (1, 0, 0, 1, 0), (0, 1, 0, 0, 0, 1), (0, 0, 0, 0, 0, 1), (0, 1, 0, 0, 0, 0),
+    (0, 0, 0, 0, 0, 0), (1, 0, 0, 0, 2), (0, 1, 1, 1, 1, 1), (1, 2, 0, 1, 2), (1, 1, 0, 1, 0), (1, 0, 0, 0, 0),
+    (0, 0, 1, 1, 1, 1), (0, 1, 1, 1, 1, 0), (1, 2, 1, 1, 2), (1, 1, 0, 0, 2), (0, 0, 1, 1, 1, 0), (1, 2, 1, 1, 1),
+    (1, 1, 1, 1, 1), (0, 1, 1, 1, 0, 1), (0, 0, 1, 1, 0, 1), (0, 1, 1, 1, 0, 0), (0, 0, 1, 1, 0, 0),
+    (1, 1, 1, 0, 1), (0, 1, 1, 0, 1, 1), (1, 2, 0, 1, 0), (0, 0, 1, 0, 1, 1), (0, 1, 1, 0, 1, 0),
+    (0, 0, 1, 0, 1, 0), (0, 1, 1, 0, 0, 1), (0, 0, 1, 0, 0, 1), (1, 1, 1, 0, 0), (0, 1, 1, 0, 0, 0),
+    (0, 0, 1, 0, 0, 0), (0, 1, 2, 1, 1, 1), (0, 0, 2, 1, 1, 1), (0, 1, 2, 1, 1, 0), (1, 0, 0, 0, 1),
+    (0, 0, 2, 1, 1, 0), (1, 2, 1, 1, 0), (1, 1, 0, 0, 1), (2, 2, 0), (3, 2, 0), (0, 1, 2, 1, 0, 1),
+    (0, 0, 2, 1, 0, 1), (0, 1, 2, 1, 0, 0), (2, 1, 0), (0, 0, 2, 1, 0, 0), (2, 0, 0), (3, 0, 0), (1, 0, 1, 1, 0),
+    (1, 2, 2, 1, 1), (3, 1, 0), (0, 1, 2, 0, 1, 1), (0, 0, 2, 0, 1, 1), (0, 1, 2, 0, 1, 0), (1, 2, 2, 0, 1),
+    (0, 0, 2, 0, 1, 0), (0, 1, 2, 0, 0, 1), (1, 2, 2, 0, 0), (0, 0, 2, 0, 0, 1), (1, 0, 2, 0, 0), (2, 2, 1),
+    (0, 1, 2, 0, 0, 0), (1, 0, 2, 1, 1), (0, 0, 2, 0, 0, 0), (0, 1, 3, 1, 1, 1), (0, 0, 3, 1, 1, 1),
+    (1, 0, 2, 0, 2), (1, 2, 2, 1, 0), (1, 0, 1, 0, 1), (0, 1, 3, 1, 1, 0), (0, 0, 3, 1, 1, 0), (0, 1, 3, 1, 0, 1),
+    (0, 0, 3, 1, 0, 1), (1, 1, 3, 0, 2), (1, 0, 2, 1, 2), (3, 2, 1), (1, 2, 2, 0, 2), (1, 2, 1, 0, 1),
+    (1, 2, 1, 0, 2), (1, 2, 2, 1, 2), (1, 0, 3, 1, 0), (0, 1, 3, 1, 0, 0), (0, 0, 3, 1, 0, 0), (1, 0, 1, 1, 1),
+    (4, 0, 0), (0, 1, 3, 0, 1, 1), (0, 0, 3, 0, 1, 1), (0, 1, 3, 0, 1, 0), (1, 2, 0, 0, 1), (1, 1, 0, 0, 0),
+    (1, 2, 3, 1, 2), (1, 1, 1, 1, 0), (0, 0, 3, 0, 1, 0), (1, 2, 3, 0, 1), (1, 2, 3, 1, 1), (0, 1, 3, 0, 0, 1),
+    (1, 1, 1, 0, 2), (4, 1, 0), (5, 1, 0), (1, 2, 0, 0, 2), (1, 2, 3, 0, 2), (0, 0, 3, 0, 0, 1), (0, 1, 3, 0, 0, 0),
+    (1, 0, 3, 0, 0), (1, 1, 1, 1, 2), (6, 1, 0), (1, 1, 2, 1, 2), (1, 0, 2, 0, 1), (5, 0, 0), (1, 0, 1, 1, 2),
+    (1, 1, 2, 0, 0), (6, 0, 0), (1, 0, 1, 0, 2), (1, 1, 2, 0, 1), (1, 0, 2, 1, 0), (1, 1, 2, 1, 1), (2, 2, 2),
+    (0, 0, 3, 0, 0, 0), (1, 2, 3, 1, 0), (1, 1, 3, 0, 1), (1, 1, 3, 1, 0), (3, 2, 2), (1, 2, 1, 0, 0),
+    (1, 1, 2, 1, 0), (2, 1, 1), (3, 1, 1), (4, 1, 1), (1, 1, 2, 0, 2), (1, 0, 1, 0, 0), (2, 1, 2), (3, 1, 2),
+    (2, 0, 1), (4, 2, 1), (5, 2, 1), (1, 1, 3, 1, 1), (2, 2, 3), (3, 2, 3), (1, 1, 3, 0, 0), (6, 2, 1),
+    (1, 0, 3, 1, 1), (3, 0, 1), (4, 2, 2), (5, 1, 1), (6, 1, 1), (5, 2, 2), (6, 2, 2), (1, 2, 0, 0, 0), (4, 1, 2),
+    (5, 1, 2), (6, 1, 2), (1, 0, 3, 1, 2), (4, 2, 0), (2, 0, 2), (3, 0, 2), (1, 1, 3, 1, 2), (4, 0, 1),
+    (1, 2, 3, 0, 0), (5, 0, 1), (6, 0, 1), (5, 2, 0), (1, 0, 3, 0, 2), (2, 0, 3), (4, 0, 2), (3, 0, 3),
+    (1, 0, 3, 0, 1), (5, 0, 2), (6, 0, 2), (4, 2, 3), (5, 2, 3), (2, 1, 3), (3, 1, 3), (6, 2, 0), (4, 1, 3),
+    (5, 1, 3), (7, 1, 0), (7, 2, 0), (4, 0, 3), (5, 0, 3), (7, 0, 0),
 )
 GATHER_ORDER = (
     (0, 2, 0), (1, 2, 1), (0, 0, 0), (3, 0, 3, 0), (1, 0, 2), (4, 2, 3, 0, 0), (1, 0, 0), (0, 1, 0), (2, 1, 3),

time: 196 us -> 194 us (0.990)
  Pallas kernels: 194 us -> 192 us
    pallas_call x1, Pallas kernels: 188 us -> 186 us  [local_step(): pl.pallas_call(functools.partial(kernel, rows), out_shape=(pltpu.VMEM(who...]
where the time goes in v8:
time: 194 us; the launch traced here: 193 us
  Pallas kernels  192 us (99%)
    pallas_call x1, Pallas kernels, local_step(): pl.pallas_call(functools.partial(kernel, rows), out_shape=(pltpu.VMEM(who...  186 us
    pallas_call x1, Pallas kernels, local_step(): pl.pallas_call(write_out, out_shape=(jax.ShapeDtypeStruct(whole, BF16), s...  6.29 us

profile of v8, /device:TPU:0, one launch (start us, length us, event | category | flops | bytes accessed | tf_op | source)
XLA Modules:
  0.0 193.2 jit_solution(876739758560887501)
XLA Ops:
  1.3 185.7 %shard_map.101 = (bf16[29376,2,128]{2,1,0:T(2,128)(2,1)S(1)}, f32[1836,128]{1,0:T(8,128)S(1)}, f32[1836,128]{1,0:T(8,128)S(1)}, f32[1836,128]{1,0:T(8,128)S(1)}, f32[1,128]{1,0:T(1,128)S(1)}) custom-call(bf16[1,7520256]{1,0:T(2,128)(2,1)} %grad_hbm.1, f32[1836,128]{1,0:T(8,128)} %bitcast.10, f32[1836,128]{1,0:T(8,128)} %bitcast.11, f32[1836,128]{1,0:T(8,128)} %bitcast.12, ...), custom_call_target="tpu_custom_call" | custom-call | tf_op jit(solution)/shard_map/pallas_call | solution.py:425
  186.9 6.3 %shard_map.102 = (bf16[29376,2,128]{2,1,0:T(2,128)(2,1)}, f32[1836,128]{1,0:T(8,128)}, f32[1836,128]{1,0:T(8,128)}, f32[1836,128]{1,0:T(8,128)}, f32[1,128]{1,0:T(1,128)}) custom-call(bf16[29376,2,128]{2,1,0:T(2,128)(2,1)S(1)} %get-tuple-element.15.refs_0_, f32[1836,128]{1,0:T(8,128)S(1)} %get-tuple-element.16.refs_1_, ...), custom_call_target="tpu_custom_call" | custom-call | tf_op jit(solution)/shard_map/pallas_call | solution.py:447
